TPU v7x, 256 devices: a whole 4x4x8 slice. The times are simulated.
256 devices in a mesh: param: 64 (over y, z, core), freq: 4 (over x).
Axes of the slice: x: 4, y: 4, z: 8, core: 2. Of those that a mesh axis runs over, the one named last changes fastest.
Arguments:
- kernel_hat: bfloat16 [2, 16, 600, 65536], P(None, 'freq', None, 'param'), may hold values from -0.25 to 0.25
- prior_gain: float32 [16, 65536], P('freq', 'param'), may hold values from 5.722046e-05 to 0.018310547, as said below
- noise_var: float32 [600], replicated, may hold values from 0.5 to 2
- observed: float32 [64, 16, 600], P('param', 'freq'), may hold values from -6 to 6
Outputs:
- solution: float32 [64, 16, 600], P('param', 'freq')
- residual: float32 [64, 16, 600], P('param', 'freq')
Inputs may be any that keep to these rules, and one draw needn't show every extreme that they name: `prior_gain`: prior variances are positive.
All inputs are finite; a program needn't handle non-finite values.
Results may differ from a plain program's by a relative error of at most 0.0085.
Values may be sent and summed in bfloat16 or wider, within the bound.
No kernel may reach another device: no remote copies, remote signals or barrier semaphores. Data moves between devices by JAX's collectives and lax.ppermute only.
A program may use at most 64 MiB of HBM per device.

v0:
```python
import math

import jax
import jax.numpy as jnp
from jax import lax
from jax.experimental import pallas as pl
from jax.experimental.pallas import tpu as pltpu
from jax.sharding import PartitionSpec as P

NT = 16
ITERS = 2
PERIOD = 2 * NT - 1

HIGHEST = lax.Precision.HIGHEST
VMEM = pltpu.VMEM
LANES = 128


def one_core_groups(count):
    return [list(range(core, count, 2)) for core in range(2)]


def from_other_core(value):
    count = lax.axis_size("param")
    return lax.ppermute(value, "param", [(i, i ^ 1) for i in range(count)])


def exchange(blocks):
    groups = one_core_groups(lax.axis_size("param"))
    return lax.all_to_all(blocks, "param", 0, 0, axis_index_groups=groups, tiled=True)


def freq_slots(value):
    length = lax.axis_size("freq")
    others = [
        lax.ppermute(value, "freq", [(i, (i + d) % length) for i in range(length)])
        for d in range(1, length)
    ]
    return (value, *others)


def slot_ids(length, each):
    mine = lax.axis_index("freq")
    slots = (mine - lax.iota(jnp.int32, length)) % length
    return (slots[:, None] * each + lax.iota(jnp.int32, each)[None, :]).reshape(-1)


def tables(freq_ids, time_ids):
    phase_int = freq_ids[:, None] * time_ids[None, :] % PERIOD
    phase = phase_int.astype(jnp.float32) * (2.0 * math.pi / PERIOD)
    return jnp.cos(phase), jnp.sin(phase)


def dot_f32(left, right):
    return jnp.dot(left, right, precision=HIGHEST, preferred_element_type=jnp.float32)


def total(value):
    return jnp.sum(jnp.sum(value, axis=0, keepdims=True), axis=1, keepdims=True)


def send_spectra(to_freq_ref, direction, out_ref):
    spectra = dot_f32(to_freq_ref[...], direction).astype(jnp.bfloat16)
    out_ref[...] = jnp.broadcast_to(spectra[None], out_ref.shape)


def first_kernel(to_freq_ref, *refs):
    *slots, out_ref = refs
    observed = jnp.concatenate([slot[...] for slot in slots], axis=0)
    send_spectra(to_freq_ref, observed, out_ref)


def applied_of(to_time_ref, noise_ref, direction, images):
    sensors = direction.shape[1]
    tiles = -(-sensors // LANES)
    each = images[0].shape[0] // tiles
    image = jnp.concatenate(
        [
            jnp.concatenate([slot[i * each : (i + 1) * each] for i in range(tiles)], axis=1)
            for slot in images
        ],
        axis=0,
    )[:, :sensors]
    return noise_ref[...] * direction + dot_f32(to_time_ref[...], image)


def middle_kernel(slots, to_freq_ref, to_time_ref, noise_ref, *refs):
    observed_refs, image_refs = refs[:slots], refs[slots : 2 * slots]
    out_ref, solution_ref, residual_ref, direction_ref, norm_ref = refs[2 * slots :]
    observed = jnp.concatenate([slot[...] for slot in observed_refs], axis=0)
    applied = applied_of(to_time_ref, noise_ref, observed, image_refs)
    norm = total(observed * observed)
    step = norm / total(observed * applied)
    residual = observed - step * applied
    fresh = total(residual * residual)
    direction = residual + (fresh / norm) * observed
    send_spectra(to_freq_ref, direction, out_ref)
    own = solution_ref.shape[0]
    solution_ref[...] = (step * observed)[:own]
    residual_ref[...] = residual[:own]
    direction_ref[...] = direction
    norm_ref[...] = jnp.broadcast_to(fresh, norm_ref.shape)


def last_kernel(to_time_ref, noise_ref, solution_ref, residual_ref, direction_ref, norm_ref, *refs):
    *image_refs, solution_out, residual_out = refs
    direction = direction_ref[...]
    applied = applied_of(to_time_ref, noise_ref, direction, image_refs)
    step = norm_ref[:1, :1] / total(direction * applied)
    own = solution_out.shape[0]
    solution_out[...] = solution_ref[...] + step * direction[:own]
    residual_out[...] = residual_ref[...] - step * applied[:own]


def hessian_kernel(slot_count, kernel_ref, gain_ref, own_ref, other_ref, own_out, other_out):
    slot = pl.program_id(0)
    rows = own_ref.shape[0]
    half = rows // (2 * slot_count)
    row = lax.broadcasted_iota(jnp.int32, (2 * half, rows), 0)
    column = lax.broadcasted_iota(jnp.int32, (2 * half, rows), 1)
    part = (row >= half).astype(jnp.int32)
    wanted = (row - part * half) * (2 * slot_count) + part * slot_count + slot
    pick = (column == wanted).astype(jnp.float32).astype(jnp.bfloat16)
    picked = [
        jnp.dot(pick, ref[...], preferred_element_type=jnp.float32).astype(jnp.bfloat16)
        for ref in (own_ref, other_ref)
    ]
    spectra = jnp.concatenate(picked, axis=0)
    real_part = kernel_ref[0, 0]
    imag_part = kernel_ref[1, 0]
    by_real = jnp.dot(spectra, real_part, preferred_element_type=jnp.float32)
    by_imag = jnp.dot(spectra, imag_part, preferred_element_type=jnp.float32)
    gain = gain_ref[pl.ds(slot, 1), :]
    coeffs = []
    for at in (0, 2 * half):
        upper, lower = slice(at, at + half), slice(at + half, at + 2 * half)
        coeffs.append(((by_real[upper] + by_imag[lower]) * gain).astype(jnp.bfloat16))
        coeffs.append(((by_real[lower] - by_imag[upper]) * gain).astype(jnp.bfloat16))
    coeffs = jnp.concatenate(coeffs, axis=0)
    contract = (((1,), (1,)), ((), ()))
    by_real = lax.dot_general(coeffs, real_part, contract, preferred_element_type=jnp.float32)
    by_imag = lax.dot_general(coeffs, imag_part, contract, preferred_element_type=jnp.float32)
    sensors = by_real.shape[1]
    tiles = -(-sensors // LANES)
    spare = jnp.zeros((half, tiles * LANES - sensors), jnp.float32)
    for at, out in ((0, own_out), (2 * half, other_out)):
        upper, lower = slice(at, at + half), slice(at + half, at + 2 * half)
        images = (by_real[upper] - by_imag[lower], by_real[lower] + by_imag[upper])
        for part, image in enumerate(images):
            image = jnp.concatenate([image, spare], axis=1)
            for tile in range(tiles):
                start = tile * 2 * slot_count + part * slot_count + slot
                out[pl.ds(start, half, stride=2 * slot_count * tiles), :] = image[
                    :, tile * LANES : (tile + 1) * LANES
                ]


def local(kernel_hat, prior_gain, noise_var, observed):
    slot_count, sensors, params = kernel_hat.shape[1:]
    own_times = observed.shape[1]
    freq_size = lax.axis_size("freq")
    half = lax.axis_size("param") // 2
    rows = half * 2 * slot_count
    block = (half, 2 * slot_count, sensors)
    image_rows = -(-sensors // LANES) * 2 * slot_count

    all_ids = slot_ids(freq_size, slot_count)
    time_ids = slot_ids(freq_size, own_times)
    out_cos, out_sin = tables(all_ids[:slot_count], time_ids)
    to_freq = jnp.concatenate([out_cos, -out_sin], axis=0)
    all_cos, all_sin = tables(all_ids, time_ids)
    both = jnp.stack(
        [
            all_cos.reshape(freq_size, slot_count, NT),
            -all_sin.reshape(freq_size, slot_count, NT),
        ],
        axis=1,
    )
    to_time = both.reshape(-1, NT).T
    noise = noise_var[None, :]

    full = pl.BlockSpec(memory_space=VMEM)

    def vmem_call(body, outs, args, name):
        return pl.pallas_call(
            body,
            out_shape=[jax.ShapeDtypeStruct(shape, dtype) for shape, dtype in outs],
            in_specs=[full] * len(args),
            out_specs=[full] * len(outs),
            name=name,
        )(*args)

    def hessian(spectra):
        own = exchange(spectra)
        other = from_other_core(own)
        whole = pl.BlockSpec((rows, sensors), lambda k: (0, 0))
        own_image, other_image = pl.pallas_call(
            lambda *refs: hessian_kernel(slot_count, *refs),
            grid=(slot_count,),
            in_specs=[
                pl.BlockSpec((2, 1, sensors, params), lambda k: (0, k, 0, 0)),
                pl.BlockSpec((slot_count, params), lambda k: (0, 0)),
                whole,
                whole,
            ],
            out_specs=[pl.BlockSpec((half * image_rows, LANES), lambda k: (0, 0))] * 2,
            out_shape=[jax.ShapeDtypeStruct((half * image_rows, LANES), jnp.float32)] * 2,
            name="hessian",
        )(
            kernel_hat,
            prior_gain,
            own.reshape(rows, sensors),
            other.reshape(rows, sensors),
        )
        arrived = from_other_core(other_image)
        partial = (own_image + arrived).reshape(half, image_rows, LANES)
        return freq_slots(exchange(partial).sum(axis=0))

    slots = freq_slots(observed[0])
    spectra = vmem_call(first_kernel, [(block, jnp.bfloat16)], (to_freq, *slots), "first")[0]
    images = hessian(spectra)
    own_shape = ((own_times, sensors), jnp.float32)
    spectra, solution, residual, direction, norm = vmem_call(
        lambda *refs: middle_kernel(freq_size, *refs),
        [
            (block, jnp.bfloat16),
            own_shape,
            own_shape,
            ((NT, sensors), jnp.float32),
            ((8, 128), jnp.float32),
        ],
        (to_freq, to_time, noise, *slots, *images),
        "middle",
    )
    images = hessian(spectra)
    solution, residual = vmem_call(
        last_kernel,
        [own_shape, own_shape],
        (to_time, noise, solution, residual, direction, norm, *images),
        "last",
    )
    return solution[None], residual[None]


def solution(mesh):
    return jax.shard_map(
        local,
        mesh=mesh,
        in_specs=(
            P(None, "freq", None, "param"),
            P("freq", "param"),
            P(),
            P("param", "freq", None),
        ),
        out_specs=(P("param", "freq", None), P("param", "freq", None)),
        check_vma=False,
    )
```

profile of v0, /device:TPU:32, one launch (start us, length us, event | category | flops | bytes accessed | tf_op | source)
XLA Modules:
  0.0 153.3 jit_solution(9923739599998527352)
XLA Ops:
  0.6 2.8 %collective-permute-start.2 = (f32[4,600]{1,0:T(4,128)}, f32[4,600]{1,0:T(4,128)S(1)}, u32[]{:S(2)}, u32[]{:S(2)}) collective-permute-start(f32[4,600]{1,0:T(4,128)} %bitcast.21), channel_id=1, source_target_pairs={{0,3},{1,0},{2,1},{3,2},{4,7},{5,4},{6,5},{7,6},{8,11},{9,8},{10,9... | collective-permute-start | bytes 28808 | tf_op jit(solution)/shard_map/ppermute | solution.py:36
  3.5 0.8 collective-permute-start.1
  4.3 0.9 collective-permute-start
  5.2 0.1 iota_add_fusion
  5.2 0.1 add.77
  5.3 0.1 fusion.11
  5.5 0.6 pad_maximum_fusion.1.to_freq_ref.refs_0_
  6.1 2.8 %collective-permute-done.1.refs_2_.refs_5_ = f32[4,600]{1,0:T(4,128)S(1)} collective-permute-done((f32[4,600]{1,0:T(4,128)}, f32[4,600]{1,0:T(4,128)S(1)}, u32[]{:S(2)}, u32[]{:S(2)}) %collective-permute-start.1) | collective-permute-done | bytes 9632 | tf_op jit(solution)/shard_map/ppermute | solution.py:36
  8.9 0.5 collective-permute-done.refs_1_.refs_4_
  9.4 0.1 copy-done.7
  9.5 0.6 copy-done.8
  10.1 1.7 %first.1 = bf16[32,8,600]{2,1,0:T(8,128)(2,1)} custom-call(f32[8,16]{1,0:T(8,128)} %pad_maximum_fusion.1.to_freq_ref.refs_0_, f32[4,600]{1,0:T(4,128)} %bitcast.24, f32[4,600]{1,0:T(4,128)} %copy-done.8, f32[4,600]{1,0:T(4,128)} %copy-done.7, f32[4,600]{1,0:T(4,128)} %copy-done.6), custom_call_target="tpu_custom_call" | custom-call | tf_op jit(solution)/shard_map/first/pallas_call | solution.py:185
  11.7 23.6 %all_to_all.20 = bf16[32,8,600]{2,1,0:T(8,128)(2,1)S(1)} all-to-all(bf16[32,8,600]{2,1,0:T(8,128)(2,1)} %first.1), channel_id=1, replica_groups={{0,8,16,24,32,40,48,56,64,72,80,88,96,104,112,120,128,136,144,152,160,1..., dimensions={0} | all-to-all | bytes 614400 | tf_op jit(solution)/shard_map/all_to_all | solution.py:30
  35.3 1.6 %collective-permute-done.3 = bf16[32,8,600]{2,1,0:T(8,128)(2,1)S(1)} collective-permute-done((bf16[32,8,600]{2,1,0:T(8,128)(2,1)S(1)}, bf16[32,8,600]{2,1,0:T(8,128)(2,1)S(1)}, u32[]{:S(2)}, u32[]{:S(2)}) %collective-permute-start.3) | collective-permute-done | bytes 307232 | tf_op jit(solution)/shard_map/ppermute | solution.py:25
  37.0 0.7 copy-done.2
  37.7 9.3 %hessian.2 = (f32[1280,128]{1,0:T(8,128)}, f32[1280,128]{1,0:T(8,128)}) custom-call(bf16[2,4,600,1024]{3,2,1,0:T(8,128)(2,1)} %refs_0_.3, f32[4,1024]{1,0:T(4,128)} %refs_1_.3, bf16[256,600]{1,0:T(8,128)(2,1)} %bitcast.14, bf16[256,600]{1,0:T(8,128)(2,1)} %bitcast.16), custom_call_target="tpu_custom_call" | custom-call | tf_op jit(solution)/shard_map/hessian/pallas_call | solution.py:197
  47.0 0.2 collective-permute-start.4
  47.1 2.1 %collective-permute-done.4 = f32[1280,128]{1,0:T(8,128)S(1)} collective-permute-done((f32[1280,128]{1,0:T(8,128)}, f32[1280,128]{1,0:T(8,128)S(1)}, u32[]{:S(2)}, u32[]{:S(2)}) %collective-permute-start.4) | collective-permute-done | bytes 655392 | tf_op jit(solution)/shard_map/ppermute | solution.py:25
  49.3 2.0 %add.80 = f32[1280,128]{1,0:T(8,128)} add(f32[1280,128]{1,0:T(8,128)} %get-tuple-element.13, f32[1280,128]{1,0:T(8,128)S(1)} %collective-permute-done.4) | non-fusion elementwise | flops 163840 | bytes 1966080 | tf_op jit(solution)/shard_map/add | solution.py:216
  51.3 4.6 %all-to-all-start.1 = ((f32[32,40,128]{2,1,0:T(8,128)}), f32[32,40,128]{2,1,0:T(8,128)S(1)}, u32[]{:S(2)}, u32[]{:S(2)}) async-start(f32[32,40,128]{2,1,0:T(8,128)} %bitcast.6), calls=%async_computation.1 | async-start | bytes 1310720 | tf_op jit(solution)/shard_map/all_to_all | solution.py:30
  55.9 0.2 fusion.5
  56.1 20.4 %all-to-all-done.1 = f32[32,40,128]{2,1,0:T(8,128)S(1)} async-done(((f32[32,40,128]{2,1,0:T(8,128)}), f32[32,40,128]{2,1,0:T(8,128)S(1)}, u32[]{:S(2)}, u32[]{:S(2)}) %all-to-all-start.1) | async-done | bytes 655392 | tf_op jit(solution)/shard_map/all_to_all | solution.py:30
  76.5 0.1 reduce_sum.18.refs_7_
  76.6 0.9 collective-permute-start.7
  77.5 0.8 collective-permute-start.6
  78.3 0.9 collective-permute-start.5
  79.2 0.6 broadcast_in_dim.6.refs_2_.noise_ref
  79.8 0.7 copy.6
  80.5 2.3 %collective-permute-done.6.refs_9_ = f32[40,128]{1,0:T(8,128)S(1)} collective-permute-done((f32[40,128]{1,0:T(8,128)S(1)}, f32[40,128]{1,0:T(8,128)S(1)}, u32[]{:S(2)}, u32[]{:S(2)}) %collective-permute-start.6) | collective-permute-done | bytes 20512 | tf_op jit(solution)/shard_map/ppermute | solution.py:36
  82.8 0.5 collective-permute-done.5.refs_8_
  83.4 0.5 copy-done.14
  83.9 2.1 %middle.1 = (bf16[32,8,600]{2,1,0:T(8,128)(2,1)}, f32[4,600]{1,0:T(4,128)}, f32[4,600]{1,0:T(4,128)}, f32[16,600]{1,0:T(8,128)}, f32[8,128]{1,0:T(8,128)}) custom-call(f32[8,16]{1,0:T(8,128)} %pad_maximum_fusion.1.to_freq_ref.refs_0_, f32[16,32]{1,0:T(8,128)} %bitcast.18, f32[1,600]{1,0:T(1,128)} %broadcast_in_dim.6.refs_2_.noise_ref, f32[4,600]{1,0:T(4,128)} %bitcast.25, ...), custom_call_target="tpu_custom_call" | custom-call | tf_op jit(solution)/shard_map/middle/pallas_call | solution.py:185
  86.0 17.1 %all_to_all.21 = bf16[32,8,600]{2,1,0:T(8,128)(2,1)S(1)} all-to-all(bf16[32,8,600]{2,1,0:T(8,128)(2,1)} %get-tuple-element.19), channel_id=1, replica_groups={{0,8,16,24,32,40,48,56,64,72,80,88,96,104,112,120,128,136,144,152,160,1..., dimensions={0} | all-to-all | bytes 614400 | tf_op jit(solution)/shard_map/all_to_all | solution.py:30
  103.1 1.6 %collective-permute-done.8 = bf16[32,8,600]{2,1,0:T(8,128)(2,1)S(1)} collective-permute-done((bf16[32,8,600]{2,1,0:T(8,128)(2,1)S(1)}, bf16[32,8,600]{2,1,0:T(8,128)(2,1)S(1)}, u32[]{:S(2)}, u32[]{:S(2)}) %collective-permute-start.8) | collective-permute-done | bytes 307232 | tf_op jit(solution)/shard_map/ppermute | solution.py:25
  104.7 0.7 copy-done.3
  105.5 9.3 %hessian.3 = (f32[1280,128]{1,0:T(8,128)}, f32[1280,128]{1,0:T(8,128)}) custom-call(bf16[2,4,600,1024]{3,2,1,0:T(8,128)(2,1)} %refs_0_.3, f32[4,1024]{1,0:T(4,128)} %refs_1_.3, bf16[256,600]{1,0:T(8,128)(2,1)} %bitcast.15, bf16[256,600]{1,0:T(8,128)(2,1)} %bitcast.17), custom_call_target="tpu_custom_call" | custom-call | tf_op jit(solution)/shard_map/hessian/pallas_call | solution.py:197
  114.7 0.1 collective-permute-start.9
  114.9 2.2 %collective-permute-done.9 = f32[1280,128]{1,0:T(8,128)S(1)} collective-permute-done((f32[1280,128]{1,0:T(8,128)}, f32[1280,128]{1,0:T(8,128)S(1)}, u32[]{:S(2)}, u32[]{:S(2)}) %collective-permute-start.9) | collective-permute-done | bytes 655392 | tf_op jit(solution)/shard_map/ppermute | solution.py:25
  117.0 1.2 add.81
  118.2 24.6 %all_to_all.22 = f32[32,40,128]{2,1,0:T(8,128)S(1)} all-to-all(f32[32,40,128]{2,1,0:T(8,128)S(1)} %bitcast.13), channel_id=1, replica_groups={{0,8,16,24,32,40,48,56,64,72,80,88,96,104,112,120,128,136,144,152,160,1..., dimensions={0} | all-to-all | bytes 1310720 | tf_op jit(solution)/shard_map/all_to_all | solution.py:30
  142.9 2.1 %collective-permute-start.12 = (f32[40,128]{1,0:T(8,128)S(1)}, f32[40,128]{1,0:T(8,128)S(1)}, u32[]{:S(2)}, u32[]{:S(2)}) collective-permute-start(f32[40,128]{1,0:T(8,128)S(1)} %reduce_sum.19.refs_0_), channel_id=1, source_target_pairs={{0,3},{1,0},{2,1},{3,2},{4,7},{5,4},{6,5},{7,6},{8,11},{9,8},{10,9... | collective-permute-start | bytes 61448 | tf_op jit(solution)/shard_map/ppermute | solution.py:36
  145.0 0.9 collective-permute-start.11
  145.9 0.2 collective-permute-start.10
  146.1 0.7 collective-permute-done.12.refs_3_
  146.8 3.6 %collective-permute-done.11.refs_2_ = f32[40,128]{1,0:T(8,128)S(1)} collective-permute-done((f32[40,128]{1,0:T(8,128)S(1)}, f32[40,128]{1,0:T(8,128)S(1)}, u32[]{:S(2)}, u32[]{:S(2)}) %collective-permute-start.11) | collective-permute-done | bytes 20512 | tf_op jit(solution)/shard_map/ppermute | solution.py:36
  150.3 0.6 collective-permute-done.10.refs_1_
  150.9 0.6 copy-done.11
  151.5 1.8 %last.1 = (f32[4,600]{1,0:T(4,128)}, f32[4,600]{1,0:T(4,128)}) custom-call(f32[16,32]{1,0:T(8,128)} %bitcast.19, f32[1,600]{1,0:T(1,128)} %broadcast_in_dim.6.refs_2_.noise_ref, f32[4,600]{1,0:T(4,128)} %get-tuple-element.15.solution_ref, f32[4,600]{1,0:T(4,128)} %get-tuple-element.16.residual_ref, f32[16,600]{1,0:T(8,128)} %get-tuple-element.17.direction_ref, ...), custom_call_target="tpu_custom_call" | custom-call | tf_op jit(solution)/shard_map/last/pallas_call | solution.py:185
  (34 shorter events, 0.2 us)
Async XLA Ops:
  0.6 78.6 %copy-start.15 = (f32[600]{0:T(1024)S(1)}, f32[600]{0:T(1024)}, u32[]{:S(2)}) copy-start(f32[600]{0:T(1024)} %param.6) | copy-start | bytes 7204
  0.6 5.4 %collective-permute-start.2 = (f32[4,600]{1,0:T(4,128)}, f32[4,600]{1,0:T(4,128)S(1)}, u32[]{:S(2)}, u32[]{:S(2)}) collective-permute-start(f32[4,600]{1,0:T(4,128)} %bitcast.21), channel_id=1, source_target_pairs={{0,3},{1,0},{2,1},{3,2},{4,7},{5,4},{6,5},{7,6},{8,11},{9,8},{10,9... | collective-permute-start | bytes 28808 | tf_op jit(solution)/shard_map/ppermute | solution.py:36
  3.5 5.4 %collective-permute-start.1 = (f32[4,600]{1,0:T(4,128)}, f32[4,600]{1,0:T(4,128)S(1)}, u32[]{:S(2)}, u32[]{:S(2)}) collective-permute-start(f32[4,600]{1,0:T(4,128)} %bitcast.22), channel_id=1, source_target_pairs={{0,2},{1,3},{2,0},{3,1},{4,6},{5,7},{6,4},{7,5},{8,10},{9,11},{10,... | collective-permute-start | bytes 28808 | tf_op jit(solution)/shard_map/ppermute | solution.py:36
  4.3 5.1 %collective-permute-start = (f32[4,600]{1,0:T(4,128)}, f32[4,600]{1,0:T(4,128)S(1)}, u32[]{:S(2)}, u32[]{:S(2)}) collective-permute-start(f32[4,600]{1,0:T(4,128)} %bitcast.23), channel_id=1, source_target_pairs={{0,1},{1,2},{2,3},{3,0},{4,5},{5,6},{6,7},{7,4},{8,9},{9,10},{10,1... | collective-permute-start | bytes 28808 | tf_op jit(solution)/shard_map/ppermute | solution.py:36
  6.1 3.3 %copy-start.6 = (f32[4,600]{1,0:T(4,128)}, f32[4,600]{1,0:T(4,128)S(1)}, u32[]{:S(2)}) copy-start(f32[4,600]{1,0:T(4,128)S(1)} %collective-permute-done.2.refs_3_.refs_6_) | copy-start | bytes 28804
  8.9 0.6 copy-start.7
  9.5 0.6 copy-start.8
  35.3 1.6 %copy-start = (bf16[32,8,600]{2,1,0:T(8,128)(2,1)}, bf16[32,8,600]{2,1,0:T(8,128)(2,1)S(1)}, u32[]{:S(2)}) copy-start(bf16[32,8,600]{2,1,0:T(8,128)(2,1)S(1)} %all_to_all.20) | copy-start | bytes 921604
  35.3 1.6 %collective-permute-start.3 = (bf16[32,8,600]{2,1,0:T(8,128)(2,1)S(1)}, bf16[32,8,600]{2,1,0:T(8,128)(2,1)S(1)}, u32[]{:S(2)}, u32[]{:S(2)}) collective-permute-start(bf16[32,8,600]{2,1,0:T(8,128)(2,1)S(1)} %all_to_all.20), channel_id=1, source_target_pairs={{0,4},{4,0},{8,12},{12,8},{16,20},{20,16},{24,28},{28,24},{32,36},... | collective-permute-start | bytes 921608 | tf_op jit(solution)/shard_map/ppermute | solution.py:25
  37.0 0.7 copy-start.2
  47.0 2.3 %collective-permute-start.4 = (f32[1280,128]{1,0:T(8,128)}, f32[1280,128]{1,0:T(8,128)S(1)}, u32[]{:S(2)}, u32[]{:S(2)}) collective-permute-start(f32[1280,128]{1,0:T(8,128)} %get-tuple-element.14), channel_id=1, source_target_pairs={{0,4},{4,0},{8,12},{12,8},{16,20},{20,16},{24,28},{28,24},{32,36},... | collective-permute-start | bytes 1966088 | tf_op jit(solution)/shard_map/ppermute | solution.py:25
  51.3 25.2 %all-to-all-start.1 = ((f32[32,40,128]{2,1,0:T(8,128)}), f32[32,40,128]{2,1,0:T(8,128)S(1)}, u32[]{:S(2)}, u32[]{:S(2)}) async-start(f32[32,40,128]{2,1,0:T(8,128)} %bitcast.6), calls=%async_computation.1 | async-start | bytes 1310720 | tf_op jit(solution)/shard_map/all_to_all | solution.py:30
  76.5 6.8 %copy-start.5 = (f32[40,128]{1,0:T(8,128)}, f32[40,128]{1,0:T(8,128)S(1)}, u32[]{:S(2)}) copy-start(f32[40,128]{1,0:T(8,128)S(1)} %reduce_sum.18.refs_7_) | copy-start | bytes 61444
  76.6 3.9 %collective-permute-start.7 = (f32[40,128]{1,0:T(8,128)S(1)}, f32[40,128]{1,0:T(8,128)S(1)}, u32[]{:S(2)}, u32[]{:S(2)}) collective-permute-start(f32[40,128]{1,0:T(8,128)S(1)} %reduce_sum.18.refs_7_), channel_id=1, source_target_pairs={{0,3},{1,0},{2,1},{3,2},{4,7},{5,4},{6,5},{7,6},{8,11},{9,8},{10,9... | collective-permute-start | bytes 61448 | tf_op jit(solution)/shard_map/ppermute | solution.py:36
  77.5 5.3 %collective-permute-start.6 = (f32[40,128]{1,0:T(8,128)S(1)}, f32[40,128]{1,0:T(8,128)S(1)}, u32[]{:S(2)}, u32[]{:S(2)}) collective-permute-start(f32[40,128]{1,0:T(8,128)S(1)} %reduce_sum.18.refs_7_), channel_id=1, source_target_pairs={{0,2},{1,3},{2,0},{3,1},{4,6},{5,7},{6,4},{7,5},{8,10},{9,11},{10,... | collective-permute-start | bytes 61448 | tf_op jit(solution)/shard_map/ppermute | solution.py:36
  78.3 5.0 %collective-permute-start.5 = (f32[40,128]{1,0:T(8,128)S(1)}, f32[40,128]{1,0:T(8,128)S(1)}, u32[]{:S(2)}, u32[]{:S(2)}) collective-permute-start(f32[40,128]{1,0:T(8,128)S(1)} %reduce_sum.18.refs_7_), channel_id=1, source_target_pairs={{0,1},{1,2},{2,3},{3,0},{4,5},{5,6},{6,7},{7,4},{8,9},{9,10},{10,1... | collective-permute-start | bytes 61448 | tf_op jit(solution)/shard_map/ppermute | solution.py:36
  80.5 2.8 %copy-start.12 = (f32[40,128]{1,0:T(8,128)}, f32[40,128]{1,0:T(8,128)S(1)}, u32[]{:S(2)}) copy-start(f32[40,128]{1,0:T(8,128)S(1)} %collective-permute-done.7.refs_10_) | copy-start | bytes 61444
  82.8 0.6 copy-start.13
  83.3 0.6 copy-start.14
  103.1 1.6 %copy-start.1 = (bf16[32,8,600]{2,1,0:T(8,128)(2,1)}, bf16[32,8,600]{2,1,0:T(8,128)(2,1)S(1)}, u32[]{:S(2)}) copy-start(bf16[32,8,600]{2,1,0:T(8,128)(2,1)S(1)} %all_to_all.21) | copy-start | bytes 921604
  103.1 1.6 %collective-permute-start.8 = (bf16[32,8,600]{2,1,0:T(8,128)(2,1)S(1)}, bf16[32,8,600]{2,1,0:T(8,128)(2,1)S(1)}, u32[]{:S(2)}, u32[]{:S(2)}) collective-permute-start(bf16[32,8,600]{2,1,0:T(8,128)(2,1)S(1)} %all_to_all.21), channel_id=1, source_target_pairs={{0,4},{4,0},{8,12},{12,8},{16,20},{20,16},{24,28},{28,24},{32,36},... | collective-permute-start | bytes 921608 | tf_op jit(solution)/shard_map/ppermute | solution.py:25
  104.7 0.7 copy-start.3
  114.7 2.3 %collective-permute-start.9 = (f32[1280,128]{1,0:T(8,128)}, f32[1280,128]{1,0:T(8,128)S(1)}, u32[]{:S(2)}, u32[]{:S(2)}) collective-permute-start(f32[1280,128]{1,0:T(8,128)} %get-tuple-element.21), channel_id=1, source_target_pairs={{0,4},{4,0},{8,12},{12,8},{16,20},{20,16},{24,28},{28,24},{32,36},... | collective-permute-start | bytes 1966088 | tf_op jit(solution)/shard_map/ppermute | solution.py:25
  142.9 8.0 %copy-start.4 = (f32[40,128]{1,0:T(8,128)}, f32[40,128]{1,0:T(8,128)S(1)}, u32[]{:S(2)}) copy-start(f32[40,128]{1,0:T(8,128)S(1)} %reduce_sum.19.refs_0_) | copy-start | bytes 61444
  142.9 3.9 %collective-permute-start.12 = (f32[40,128]{1,0:T(8,128)S(1)}, f32[40,128]{1,0:T(8,128)S(1)}, u32[]{:S(2)}, u32[]{:S(2)}) collective-permute-start(f32[40,128]{1,0:T(8,128)S(1)} %reduce_sum.19.refs_0_), channel_id=1, source_target_pairs={{0,3},{1,0},{2,1},{3,2},{4,7},{5,4},{6,5},{7,6},{8,11},{9,8},{10,9... | collective-permute-start | bytes 61448 | tf_op jit(solution)/shard_map/ppermute | solution.py:36
  145.0 5.3 %collective-permute-start.11 = (f32[40,128]{1,0:T(8,128)S(1)}, f32[40,128]{1,0:T(8,128)S(1)}, u32[]{:S(2)}, u32[]{:S(2)}) collective-permute-start(f32[40,128]{1,0:T(8,128)S(1)} %reduce_sum.19.refs_0_), channel_id=1, source_target_pairs={{0,2},{1,3},{2,0},{3,1},{4,6},{5,7},{6,4},{7,5},{8,10},{9,11},{10,... | collective-permute-start | bytes 61448 | tf_op jit(solution)/shard_map/ppermute | solution.py:36
  145.9 5.0 %collective-permute-start.10 = (f32[40,128]{1,0:T(8,128)S(1)}, f32[40,128]{1,0:T(8,128)S(1)}, u32[]{:S(2)}, u32[]{:S(2)}) collective-permute-start(f32[40,128]{1,0:T(8,128)S(1)} %reduce_sum.19.refs_0_), channel_id=1, source_target_pairs={{0,1},{1,2},{2,3},{3,0},{4,5},{5,6},{6,7},{7,4},{8,9},{9,10},{10,1... | collective-permute-start | bytes 61448 | tf_op jit(solution)/shard_map/ppermute | solution.py:36
  146.8 4.1 %copy-start.9 = (f32[40,128]{1,0:T(8,128)}, f32[40,128]{1,0:T(8,128)S(1)}, u32[]{:S(2)}) copy-start(f32[40,128]{1,0:T(8,128)S(1)} %collective-permute-done.12.refs_3_) | copy-start | bytes 61444
  150.3 0.6 copy-start.10
  150.9 0.6 copy-start.11
where the time goes:
time: 154 us; the launch traced here: 153 us
  blocking collectives  65.3 us (42%)
  waiting for transfers between devices  38.9 us (25%)
  Pallas kernels  24.1 us (16%)
  starting transfers between devices  15.3 us (10%)
  local copies, waits for them, and re-layouts  4.68 us (3%)
  other arithmetic  4.29 us (3%)
    all_to_all x3, blocking collectives, exchange(): lax.all_to_all(blocks, 'param', 0, 0, axis_index_groups=groups, tiled=True)  65.3 us
    all_to_all x1, waiting for transfers between devices, exchange(): lax.all_to_all(blocks, 'param', 0, 0, axis_index_groups=groups, tiled=True)  20.4 us
    pallas_call x2, Pallas kernels, hessian(): pl.pallas_call(lambda *refs: hessian_kernel(slot_count, *refs), grid=(slo...  18.5 us
    ppermute x9, waiting for transfers between devices, freq_slots(): lax.ppermute(value, 'freq', [(i, (i + d) % length) for i in range(length)])  10.9 us
    ppermute x9, starting transfers between devices, freq_slots(): lax.ppermute(value, 'freq', [(i, (i + d) % length) for i in range(length)])  10.4 us
    ppermute x4, waiting for transfers between devices, from_other_core(): return lax.ppermute(value, 'param', [(i, i ^ 1) for i in range(count)])  7.57 us
    pallas_call x3, Pallas kernels, vmem_call(): pl.pallas_call(body, out_shape=[jax.ShapeDtypeStruct(shape, dtype) for sh...  5.57 us
    all_to_all x1, starting transfers between devices, exchange(): lax.all_to_all(blocks, 'param', 0, 0, axis_index_groups=groups, tiled=True)  4.58 us
  transfers between devices with their start and end apart: 14, of which 12 were waited for; matrix products, arithmetic and copies ran while one was open for 2% of the time, Pallas kernels for 0%

commit v1 on v0

v1 whole, which is shorter than its diff:
```python
import math

import jax
import jax.numpy as jnp
from jax import lax
from jax.experimental import pallas as pl
from jax.experimental.pallas import tpu as pltpu
from jax.sharding import PartitionSpec as P

NT = 16
ITERS = 2
PERIOD = 2 * NT - 1

HIGHEST = lax.Precision.HIGHEST
VMEM = pltpu.VMEM
LANES = 128
MIB = 1024 * 1024


def one_core_groups(count):
    return [list(range(core, count, 2)) for core in range(2)]


def from_other_core(value):
    count = lax.axis_size("param")
    return lax.ppermute(value, "param", [(i, i ^ 1) for i in range(count)])


def exchange(blocks):
    groups = one_core_groups(lax.axis_size("param"))
    return lax.all_to_all(blocks, "param", 0, 0, axis_index_groups=groups, tiled=True)


def freq_slots(value):
    length = lax.axis_size("freq")
    others = [
        lax.ppermute(value, "freq", [(i, (i + d) % length) for i in range(length)])
        for d in range(1, length)
    ]
    return (value, *others)


def true_id(place, each):
    length = lax.axis_size("freq")
    slot = (lax.axis_index("freq") + length - place // each) % length
    return slot * each + place % each


def phase_table(freq_ids, time_ids, part):
    phase_int = freq_ids * time_ids % PERIOD
    phase = phase_int.astype(jnp.float32) * (2.0 * math.pi / PERIOD)
    return jnp.where(part == 0, jnp.cos(phase), -jnp.sin(phase))


def iota(shape, dim):
    return lax.broadcasted_iota(jnp.int32, shape, dim)


def dot_f32(left, right):
    return jnp.dot(left, right, precision=HIGHEST, preferred_element_type=jnp.float32)


def total(value):
    return jnp.sum(jnp.sum(value, axis=0, keepdims=True), axis=1, keepdims=True)


def send_spectra(to_freq_ref, direction, out_ref):
    spectra = dot_f32(to_freq_ref[...], direction).astype(jnp.bfloat16)
    out_ref[...] = jnp.broadcast_to(spectra[None], out_ref.shape)


def first_kernel(_, to_freq_ref, *refs):
    *slots, out_ref = refs
    observed = jnp.concatenate([slot[...] for slot in slots], axis=0)
    send_spectra(to_freq_ref, observed, out_ref)


def applied_of(to_time_ref, noise_ref, direction, images):
    sensors = direction.shape[1]
    tiles = -(-sensors // LANES)
    each = images[0].shape[0] // tiles
    image = jnp.concatenate(
        [
            jnp.concatenate([slot[i * each : (i + 1) * each] for i in range(tiles)], axis=1)
            for slot in images
        ],
        axis=0,
    )[:, :sensors]
    return noise_ref[...] * direction + dot_f32(to_time_ref[...], image)


def middle_kernel(slots, to_freq_ref, to_time_ref, noise_ref, *refs):
    observed_refs, image_refs = refs[:slots], refs[slots : 2 * slots]
    out_ref, solution_ref, residual_ref, direction_ref, norm_ref = refs[2 * slots :]
    observed = jnp.concatenate([slot[...] for slot in observed_refs], axis=0)
    applied = applied_of(to_time_ref, noise_ref, observed, image_refs)
    norm = total(observed * observed)
    step = norm / total(observed * applied)
    residual = observed - step * applied
    fresh = total(residual * residual)
    direction = residual + (fresh / norm) * observed
    send_spectra(to_freq_ref, direction, out_ref)
    own = solution_ref.shape[0]
    solution_ref[...] = (step * observed)[:own]
    residual_ref[...] = residual[:own]
    direction_ref[...] = direction
    norm_ref[...] = jnp.broadcast_to(fresh, norm_ref.shape)


def last_kernel(to_time_ref, noise_ref, solution_ref, residual_ref, direction_ref, norm_ref, *refs):
    *image_refs, solution_out, residual_out = refs
    direction = direction_ref[...]
    applied = applied_of(to_time_ref, noise_ref, direction, image_refs)
    step = norm_ref[:1, :1] / total(direction * applied)
    own = solution_out.shape[0]
    solution_out[...] = solution_ref[...] + step * direction[:own]
    residual_out[...] = residual_ref[...] - step * applied[:own]


def touch_kernel(*refs):
    out = refs[-1]
    out[...] = jnp.zeros_like(out)


def hessian_kernel(slot_count, kernel_ref, gain_ref, own_ref, other_ref, own_out, other_out):
    rows, sensors = own_ref.shape
    both = rows // slot_count
    half = both // 2
    tiles = -(-sensors // LANES)
    spare = jnp.zeros((half, tiles * LANES - sensors), jnp.float32)
    row = lax.broadcasted_iota(jnp.int32, (rows, rows), 0)
    column = lax.broadcasted_iota(jnp.int32, (rows, rows), 1)
    wanted = row % half * (2 * slot_count) + row // half % 2 * slot_count + row // both
    pick = (column == wanted).astype(jnp.float32).astype(jnp.bfloat16)
    own, other = [
        jnp.dot(pick, ref[...], preferred_element_type=jnp.float32).astype(jnp.bfloat16)
        for ref in (own_ref, other_ref)
    ]
    contract = (((1,), (1,)), ((), ()))

    def forward(slot):
        at = slice(slot * both, (slot + 1) * both)
        spectra = jnp.concatenate([own[at], other[at]], axis=0)
        by_real = jnp.dot(spectra, kernel_ref[0, slot], preferred_element_type=jnp.float32)
        by_imag = jnp.dot(spectra, kernel_ref[1, slot], preferred_element_type=jnp.float32)
        gain = gain_ref[slot : slot + 1, :]
        coeffs = []
        for at in (0, both):
            upper, lower = slice(at, at + half), slice(at + half, at + both)
            coeffs.append(((by_real[upper] + by_imag[lower]) * gain).astype(jnp.bfloat16))
            coeffs.append(((by_real[lower] - by_imag[upper]) * gain).astype(jnp.bfloat16))
        return jnp.concatenate(coeffs, axis=0)

    def backward(slot, coeffs):
        by_real, by_imag = [
            lax.dot_general(
                coeffs, kernel_ref[part, slot], contract, preferred_element_type=jnp.float32
            )
            for part in range(2)
        ]
        for at, out in ((0, own_out), (both, other_out)):
            upper, lower = slice(at, at + half), slice(at + half, at + both)
            images = (by_real[upper] - by_imag[lower], by_real[lower] + by_imag[upper])
            for part, image in enumerate(images):
                image = jnp.concatenate([image, spare], axis=1)
                for tile in range(tiles):
                    start = tile * 2 * slot_count + part * slot_count + slot
                    out[pl.ds(start, half, stride=2 * slot_count * tiles), :] = image[
                        :, tile * LANES : (tile + 1) * LANES
                    ]

    coeffs = forward(0)
    for slot in range(slot_count):
        following = forward(slot + 1) if slot + 1 < slot_count else None
        backward(slot, coeffs)
        coeffs = following


def local(kernel_hat, prior_gain, noise_var, observed):
    slot_count, sensors, params = kernel_hat.shape[1:]
    own_times = observed.shape[1]
    freq_size = lax.axis_size("freq")
    half = lax.axis_size("param") // 2
    rows = half * 2 * slot_count
    block = (half, 2 * slot_count, sensors)
    image_rows = -(-sensors // LANES) * 2 * slot_count

    spectral = 2 * slot_count
    shape = (spectral, NT)
    row = iota(shape, 0)
    to_freq = phase_table(
        true_id(row % slot_count, slot_count),
        true_id(iota(shape, 1), own_times),
        row // slot_count,
    )
    shape = (NT, freq_size * spectral)
    column = iota(shape, 1)
    to_time = phase_table(
        true_id(column // spectral * slot_count + column % slot_count, slot_count),
        true_id(iota(shape, 0), own_times),
        column % spectral // slot_count,
    )
    noise = noise_var[None, :]

    full = pl.BlockSpec(memory_space=VMEM)

    def vmem_call(body, outs, args, name, limit=4, cost=None):
        return pl.pallas_call(
            body,
            out_shape=[jax.ShapeDtypeStruct(shape, dtype) for shape, dtype in outs],
            in_specs=[full] * len(args),
            out_specs=[full] * len(outs),
            compiler_params=pltpu.CompilerParams(vmem_limit_bytes=limit * MIB),
            cost_estimate=cost,
            name=name,
        )(*args)

    def hessian(spectra):
        own = exchange(spectra)
        other = from_other_core(own)
        own_image, other_image = vmem_call(
            lambda *refs: hessian_kernel(slot_count, *refs),
            [((half * image_rows, LANES), jnp.float32)] * 2,
            (
                kernel_hat,
                prior_gain,
                own.reshape(rows, sensors),
                other.reshape(rows, sensors),
            ),
            "hessian",
            16,
        )
        arrived = from_other_core(other_image)
        partial = (own_image + arrived).astype(jnp.bfloat16)
        partials = exchange(partial.reshape(half, image_rows, LANES))
        return freq_slots(partials.astype(jnp.float32).sum(axis=0))

    slots = freq_slots(observed[0])
    touched = vmem_call(
        touch_kernel,
        [((8, 128), jnp.float32)],
        (kernel_hat, to_freq, to_time, noise),
        "touch",
        4,
        pl.CostEstimate(flops=10**10, bytes_accessed=10**7, transcendentals=0),
    )[0]
    spectra = vmem_call(first_kernel, [(block, jnp.bfloat16)], (touched, to_freq, *slots), "first")[0]
    images = hessian(spectra)
    own_shape = ((own_times, sensors), jnp.float32)
    spectra, solution, residual, direction, norm = vmem_call(
        lambda *refs: middle_kernel(freq_size, *refs),
        [
            (block, jnp.bfloat16),
            own_shape,
            own_shape,
            ((NT, sensors), jnp.float32),
            ((8, 128), jnp.float32),
        ],
        (to_freq, to_time, noise, *slots, *images),
        "middle",
    )
    images = hessian(spectra)
    solution, residual = vmem_call(
        last_kernel,
        [own_shape, own_shape],
        (to_time, noise, solution, residual, direction, norm, *images),
        "last",
    )
    return solution[None], residual[None]


def solution(mesh):
    return jax.shard_map(
        local,
        mesh=mesh,
        in_specs=(
            P(None, "freq", None, "param"),
            P("freq", "param"),
            P(),
            P("param", "freq", None),
        ),
        out_specs=(P("param", "freq", None), P("param", "freq", None)),
        check_vma=False,
    )
```

time: 154 us -> 124 us (0.81)
  waiting for transfers between devices: 38.9 us -> 16.4 us
  blocking collectives: 65.3 us -> 77 us
  Pallas kernels: 24.1 us -> 12.5 us
  starting transfers between devices: 15.3 us -> 11.2 us
  other arithmetic: 4.29 us -> 0.6 us
    all_to_all x1 -> x0, waiting for transfers between devices: 20.4 us -> none  [exchange(): lax.all_to_all(blocks, 'param', 0, 0, axis_index_groups=groups, tiled=True)]
    pallas_call x2 -> x0, Pallas kernels: 18.5 us -> none  [hessian(): pl.pallas_call(lambda *refs: hessian_kernel(slot_count, *refs), grid=(slo...]
    all_to_all x3 -> x4, blocking collectives: 65.3 us -> 77 us  [exchange(): lax.all_to_all(blocks, 'param', 0, 0, axis_index_groups=groups, tiled=True)]
    pallas_call x3 -> x6, Pallas kernels: 5.57 us -> 12.5 us  [vmem_call(): pl.pallas_call(body, out_shape=[jax.ShapeDtypeStruct(shape, dtype) for sh...]
    all_to_all x1 -> x0, starting transfers between devices: 4.58 us -> none  [exchange(): lax.all_to_all(blocks, 'param', 0, 0, axis_index_groups=groups, tiled=True)]
    add x3 -> x2, other arithmetic: 3.27 us -> 0.01 us  [the longest x1 0.01 us: local(): row % slot_count]
    ppermute x9, waiting for transfers between devices: 10.9 us -> 9.27 us  [freq_slots(): lax.ppermute(value, 'freq', [(i, (i + d) % length) for i in range(length)])]
    unnamed x32 -> x8, local copies, waits for them, and re-layouts: 3.35 us -> 4.46 us
  transfers between devices with their start and end apart: 14 -> 13, of which waited for: 12 -> 9; matrix products, arithmetic and copies ran while one was open for 2% -> 1% of each run, Pallas kernels for 0% -> 0%
where the time goes in v1:
time: 124 us
  blocking collectives  77 us (62%)
  waiting for transfers between devices  16.4 us (13%)
  Pallas kernels  12.5 us (10%)
  starting transfers between devices  11.2 us (9%)
  local copies, waits for them, and re-layouts  5.15 us (4%)
    all_to_all x4, blocking collectives, exchange(): lax.all_to_all(blocks, 'param', 0, 0, axis_index_groups=groups, tiled=True)  77 us
    pallas_call x6, Pallas kernels, vmem_call(): pl.pallas_call(body, out_shape=[jax.ShapeDtypeStruct(shape, dtype) for sh...  12.5 us
    ppermute x9, starting transfers between devices, freq_slots(): lax.ppermute(value, 'freq', [(i, (i + d) % length) for i in range(length)])  10.7 us
    ppermute x9, waiting for transfers between devices, freq_slots(): lax.ppermute(value, 'freq', [(i, (i + d) % length) for i in range(length)])  9.27 us
    ppermute x4, waiting for transfers between devices, from_other_core(): return lax.ppermute(value, 'param', [(i, i ^ 1) for i in range(count)])  7.17 us
    unnamed x8, local copies, waits for them, and re-layouts  4.46 us
  transfers between devices with their start and end apart: 13, of which 9 were waited for; matrix products, arithmetic and copies ran while one was open for 1% of the time, Pallas kernels for 0%

profile of v1, /device:TPU:32, one launch (start us, length us, event | category | flops | bytes accessed | tf_op | source)
XLA Modules:
  0.0 123.7 jit_solution(10989247309955809143)
XLA Ops:
  0.6 2.8 %collective-permute-start.2 = (f32[4,600]{1,0:T(4,128)}, f32[4,600]{1,0:T(4,128)S(1)}, u32[]{:S(2)}, u32[]{:S(2)}) collective-permute-start(f32[4,600]{1,0:T(4,128)} %bitcast.13), channel_id=1, source_target_pairs={{0,3},{1,0},{2,1},{3,2},{4,7},{5,4},{6,5},{7,6},{8,11},{9,8},{10,9... | collective-permute-start | bytes 28808 | tf_op jit(solution)/shard_map/ppermute | solution.py:37
  3.5 0.8 collective-permute-start.1
  4.3 0.9 collective-permute-start
  5.3 0.7 broadcast_in_dim.9.refs_3_.refs_2_.noise_ref
  6.0 0.1 negate_select_fusion.16.refs_1_.to_freq_ref.refs_0_
  6.1 0.1 negate_select_fusion.9.refs_2_.refs_1_.to_time_ref
  6.3 0.0 copy-start
  6.3 3.8 %copy-done = bf16[2,4,600,1024]{3,2,1,0:T(8,128)(2,1)S(1)} copy-done((bf16[2,4,600,1024]{3,2,1,0:T(8,128)(2,1)S(1)}, bf16[2,4,600,1024]{3,2,1,0:T(8,128)(2,1)}, u32[]{:S(2)}) %copy-start) | copy-done | bytes 9830424
  10.0 0.0 copy-start.3
  10.1 0.0 collective-permute-done.2.refs_3_.refs_6_
  10.1 0.0 collective-permute-done.1.refs_2_.refs_5_
  10.1 0.0 collective-permute-done.refs_1_.refs_4_
  10.1 0.7 copy-done.3
  10.7 0.2 first.1
  10.9 24.2 %all_to_all.20 = bf16[32,8,600]{2,1,0:T(8,128)(2,1)S(1)} all-to-all(bf16[32,8,600]{2,1,0:T(8,128)(2,1)S(1)} %first.1), channel_id=1, replica_groups={{0,8,16,24,32,40,48,56,64,72,80,88,96,104,112,120,128,136,144,152,160,1..., dimensions={0} | all-to-all | bytes 614400 | tf_op jit(solution)/shard_map/all_to_all | solution.py:31
  35.1 0.0 collective-permute-start.3
  35.1 1.6 %collective-permute-done.3 = bf16[32,8,600]{2,1,0:T(8,128)(2,1)S(1)} collective-permute-done((bf16[32,8,600]{2,1,0:T(8,128)(2,1)S(1)}, bf16[32,8,600]{2,1,0:T(8,128)(2,1)S(1)}, u32[]{:S(2)}, u32[]{:S(2)}) %collective-permute-start.3) | collective-permute-done | bytes 307232 | tf_op jit(solution)/shard_map/ppermute | solution.py:26
  36.7 0.0 copy-done.1
  36.7 0.0 copy-done.2
  36.7 5.4 %hessian.2 = (f32[1280,128]{1,0:T(8,128)S(1)}, f32[1280,128]{1,0:T(8,128)S(1)}) custom-call(bf16[2,4,600,1024]{3,2,1,0:T(8,128)(2,1)S(1)} %copy-done.1, f32[4,1024]{1,0:T(4,128)S(1)} %copy-done.2, bf16[256,600]{1,0:T(8,128)(2,1)S(1)} %bitcast.9, bf16[256,600]{1,0:T(8,128)(2,1)S(1)} %bitcast.11), custom_call_target="tpu_custom_call" | custom-call | tf_op jit(solution)/shard_map/hessian/pallas_call | solution.py:208
  42.2 0.2 collective-permute-start.4
  42.4 2.0 %collective-permute-done.4 = f32[1280,128]{1,0:T(8,128)S(1)} collective-permute-done((f32[1280,128]{1,0:T(8,128)S(1)}, f32[1280,128]{1,0:T(8,128)S(1)}, u32[]{:S(2)}, u32[]{:S(2)}) %collective-permute-start.4) | collective-permute-done | bytes 655392 | tf_op jit(solution)/shard_map/ppermute | solution.py:26
  44.4 0.1 add_convert_fusion.1
  44.4 18.4 %all_to_all.21 = bf16[32,40,128]{2,1,0:T(8,128)(2,1)S(1)} all-to-all(bf16[32,40,128]{2,1,0:T(8,128)(2,1)S(1)} %bitcast.18), channel_id=1, replica_groups={{0,8,16,24,32,40,48,56,64,72,80,88,96,104,112,120,128,136,144,152,160,1..., dimensions={0} | all-to-all | bytes 655360 | tf_op jit(solution)/shard_map/all_to_all | solution.py:31
  62.8 0.1 convert_reduce_fusion.1.refs_7_
  62.9 2.4 %collective-permute-start.7 = (f32[40,128]{1,0:T(8,128)S(1)}, f32[40,128]{1,0:T(8,128)S(1)}, u32[]{:S(2)}, u32[]{:S(2)}) collective-permute-start(f32[40,128]{1,0:T(8,128)S(1)} %convert_reduce_fusion.1.refs_7_), channel_id=1, source_target_pairs={{0,3},{1,0},{2,1},{3,2},{4,7},{5,4},{6,5},{7,6},{8,11},{9,8},{10,9... | collective-permute-start | bytes 61448 | tf_op jit(solution)/shard_map/ppermute | solution.py:37
  65.3 1.5 %collective-permute-start.6 = (f32[40,128]{1,0:T(8,128)S(1)}, f32[40,128]{1,0:T(8,128)S(1)}, u32[]{:S(2)}, u32[]{:S(2)}) collective-permute-start(f32[40,128]{1,0:T(8,128)S(1)} %convert_reduce_fusion.1.refs_7_), channel_id=1, source_target_pairs={{0,2},{1,3},{2,0},{3,1},{4,6},{5,7},{6,4},{7,5},{8,10},{9,11},{10,... | collective-permute-start | bytes 61448 | tf_op jit(solution)/shard_map/ppermute | solution.py:37
  66.8 0.0 collective-permute-start.5
  66.8 0.0 collective-permute-done.7.refs_10_
  66.8 3.8 %collective-permute-done.6.refs_9_ = f32[40,128]{1,0:T(8,128)S(1)} collective-permute-done((f32[40,128]{1,0:T(8,128)S(1)}, f32[40,128]{1,0:T(8,128)S(1)}, u32[]{:S(2)}, u32[]{:S(2)}) %collective-permute-start.6) | collective-permute-done | bytes 20512 | tf_op jit(solution)/shard_map/ppermute | solution.py:37
  70.6 1.2 collective-permute-done.5.refs_8_
  71.8 0.6 middle.1
  72.4 16.6 %all_to_all.22 = bf16[32,8,600]{2,1,0:T(8,128)(2,1)S(1)} all-to-all(bf16[32,8,600]{2,1,0:T(8,128)(2,1)S(1)} %get-tuple-element.19), channel_id=1, replica_groups={{0,8,16,24,32,40,48,56,64,72,80,88,96,104,112,120,128,136,144,152,160,1..., dimensions={0} | all-to-all | bytes 614400 | tf_op jit(solution)/shard_map/all_to_all | solution.py:31
  88.9 0.0 collective-permute-start.8
  88.9 1.6 %collective-permute-done.8 = bf16[32,8,600]{2,1,0:T(8,128)(2,1)S(1)} collective-permute-done((bf16[32,8,600]{2,1,0:T(8,128)(2,1)S(1)}, bf16[32,8,600]{2,1,0:T(8,128)(2,1)S(1)}, u32[]{:S(2)}, u32[]{:S(2)}) %collective-permute-start.8) | collective-permute-done | bytes 307232 | tf_op jit(solution)/shard_map/ppermute | solution.py:26
  90.6 5.4 %hessian.3 = (f32[1280,128]{1,0:T(8,128)S(1)}, f32[1280,128]{1,0:T(8,128)S(1)}) custom-call(bf16[2,4,600,1024]{3,2,1,0:T(8,128)(2,1)S(1)} %copy-done.1, f32[4,1024]{1,0:T(4,128)S(1)} %copy-done.2, bf16[256,600]{1,0:T(8,128)(2,1)S(1)} %bitcast.10, bf16[256,600]{1,0:T(8,128)(2,1)S(1)} %bitcast.12), custom_call_target="tpu_custom_call" | custom-call | tf_op jit(solution)/shard_map/hessian/pallas_call | solution.py:208
  96.0 0.2 collective-permute-start.9
  96.2 1.9 %collective-permute-done.9 = f32[1280,128]{1,0:T(8,128)S(1)} collective-permute-done((f32[1280,128]{1,0:T(8,128)S(1)}, f32[1280,128]{1,0:T(8,128)S(1)}, u32[]{:S(2)}, u32[]{:S(2)}) %collective-permute-start.9) | collective-permute-done | bytes 655392 | tf_op jit(solution)/shard_map/ppermute | solution.py:26
  98.2 0.1 add_convert_fusion
  98.2 17.9 %all_to_all.23 = bf16[32,40,128]{2,1,0:T(8,128)(2,1)S(1)} all-to-all(bf16[32,40,128]{2,1,0:T(8,128)(2,1)S(1)} %bitcast.19), channel_id=1, replica_groups={{0,8,16,24,32,40,48,56,64,72,80,88,96,104,112,120,128,136,144,152,160,1..., dimensions={0} | all-to-all | bytes 655360 | tf_op jit(solution)/shard_map/all_to_all | solution.py:31
  116.2 0.1 convert_reduce_fusion.refs_0_
  116.2 0.2 collective-permute-start.12
  116.4 1.2 collective-permute-start.11
  117.6 0.9 collective-permute-start.10
  118.5 1.6 %collective-permute-done.12.refs_3_ = f32[40,128]{1,0:T(8,128)S(1)} collective-permute-done((f32[40,128]{1,0:T(8,128)S(1)}, f32[40,128]{1,0:T(8,128)S(1)}, u32[]{:S(2)}, u32[]{:S(2)}) %collective-permute-start.12) | collective-permute-done | bytes 20512 | tf_op jit(solution)/shard_map/ppermute | solution.py:37
  120.1 1.6 %collective-permute-done.11.refs_2_ = f32[40,128]{1,0:T(8,128)S(1)} collective-permute-done((f32[40,128]{1,0:T(8,128)S(1)}, f32[40,128]{1,0:T(8,128)S(1)}, u32[]{:S(2)}, u32[]{:S(2)}) %collective-permute-start.11) | collective-permute-done | bytes 20512 | tf_op jit(solution)/shard_map/ppermute | solution.py:37
  121.7 1.1 collective-permute-done.10.refs_1_
  122.8 0.9 last.1
  (14 shorter events, 0.1 us)
Async XLA Ops:
  0.6 9.4 %collective-permute-start.2 = (f32[4,600]{1,0:T(4,128)}, f32[4,600]{1,0:T(4,128)S(1)}, u32[]{:S(2)}, u32[]{:S(2)}) collective-permute-start(f32[4,600]{1,0:T(4,128)} %bitcast.13), channel_id=1, source_target_pairs={{0,3},{1,0},{2,1},{3,2},{4,7},{5,4},{6,5},{7,6},{8,11},{9,8},{10,9... | collective-permute-start | bytes 28808 | tf_op jit(solution)/shard_map/ppermute | solution.py:37
  3.5 6.6 %collective-permute-start.1 = (f32[4,600]{1,0:T(4,128)}, f32[4,600]{1,0:T(4,128)S(1)}, u32[]{:S(2)}, u32[]{:S(2)}) collective-permute-start(f32[4,600]{1,0:T(4,128)} %bitcast.14), channel_id=1, source_target_pairs={{0,2},{1,3},{2,0},{3,1},{4,6},{5,7},{6,4},{7,5},{8,10},{9,11},{10,... | collective-permute-start | bytes 28808 | tf_op jit(solution)/shard_map/ppermute | solution.py:37
  4.3 5.8 %collective-permute-start = (f32[4,600]{1,0:T(4,128)}, f32[4,600]{1,0:T(4,128)S(1)}, u32[]{:S(2)}, u32[]{:S(2)}) collective-permute-start(f32[4,600]{1,0:T(4,128)} %bitcast.15), channel_id=1, source_target_pairs={{0,1},{1,2},{2,3},{3,0},{4,5},{5,6},{6,7},{7,4},{8,9},{9,10},{10,1... | collective-permute-start | bytes 28808 | tf_op jit(solution)/shard_map/ppermute | solution.py:37
  6.3 3.8 %copy-start = (bf16[2,4,600,1024]{3,2,1,0:T(8,128)(2,1)S(1)}, bf16[2,4,600,1024]{3,2,1,0:T(8,128)(2,1)}, u32[]{:S(2)}) copy-start(bf16[2,4,600,1024]{3,2,1,0:T(8,128)(2,1)} %refs_0_.5) | copy-start | bytes 29491204
  10.0 0.7 copy-start.3
  10.0 26.7 %copy-start.1 = (bf16[2,4,600,1024]{3,2,1,0:T(8,128)(2,1)S(1)}, bf16[2,4,600,1024]{3,2,1,0:T(8,128)(2,1)}, u32[]{:S(2)}) copy-start(bf16[2,4,600,1024]{3,2,1,0:T(8,128)(2,1)} %refs_0_.5) | copy-start | bytes 29491204
  10.1 26.7 %copy-start.2 = (f32[4,1024]{1,0:T(4,128)S(1)}, f32[4,1024]{1,0:T(4,128)}, u32[]{:S(2)}) copy-start(f32[4,1024]{1,0:T(4,128)} %refs_1_.3) | copy-start | bytes 49156
  35.1 1.6 %collective-permute-start.3 = (bf16[32,8,600]{2,1,0:T(8,128)(2,1)S(1)}, bf16[32,8,600]{2,1,0:T(8,128)(2,1)S(1)}, u32[]{:S(2)}, u32[]{:S(2)}) collective-permute-start(bf16[32,8,600]{2,1,0:T(8,128)(2,1)S(1)} %all_to_all.20), channel_id=1, source_target_pairs={{0,4},{4,0},{8,12},{12,8},{16,20},{20,16},{24,28},{28,24},{32,36},... | collective-permute-start | bytes 921608 | tf_op jit(solution)/shard_map/ppermute | solution.py:26
  42.2 2.2 %collective-permute-start.4 = (f32[1280,128]{1,0:T(8,128)S(1)}, f32[1280,128]{1,0:T(8,128)S(1)}, u32[]{:S(2)}, u32[]{:S(2)}) collective-permute-start(f32[1280,128]{1,0:T(8,128)S(1)} %get-tuple-element.14), channel_id=1, source_target_pairs={{0,4},{4,0},{8,12},{12,8},{16,20},{20,16},{24,28},{28,24},{32,36},... | collective-permute-start | bytes 1966088 | tf_op jit(solution)/shard_map/ppermute | solution.py:26
  62.9 3.9 %collective-permute-start.7 = (f32[40,128]{1,0:T(8,128)S(1)}, f32[40,128]{1,0:T(8,128)S(1)}, u32[]{:S(2)}, u32[]{:S(2)}) collective-permute-start(f32[40,128]{1,0:T(8,128)S(1)} %convert_reduce_fusion.1.refs_7_), channel_id=1, source_target_pairs={{0,3},{1,0},{2,1},{3,2},{4,7},{5,4},{6,5},{7,6},{8,11},{9,8},{10,9... | collective-permute-start | bytes 61448 | tf_op jit(solution)/shard_map/ppermute | solution.py:37
  65.3 5.3 %collective-permute-start.6 = (f32[40,128]{1,0:T(8,128)S(1)}, f32[40,128]{1,0:T(8,128)S(1)}, u32[]{:S(2)}, u32[]{:S(2)}) collective-permute-start(f32[40,128]{1,0:T(8,128)S(1)} %convert_reduce_fusion.1.refs_7_), channel_id=1, source_target_pairs={{0,2},{1,3},{2,0},{3,1},{4,6},{5,7},{6,4},{7,5},{8,10},{9,11},{10,... | collective-permute-start | bytes 61448 | tf_op jit(solution)/shard_map/ppermute | solution.py:37
  66.8 5.0 %collective-permute-start.5 = (f32[40,128]{1,0:T(8,128)S(1)}, f32[40,128]{1,0:T(8,128)S(1)}, u32[]{:S(2)}, u32[]{:S(2)}) collective-permute-start(f32[40,128]{1,0:T(8,128)S(1)} %convert_reduce_fusion.1.refs_7_), channel_id=1, source_target_pairs={{0,1},{1,2},{2,3},{3,0},{4,5},{5,6},{6,7},{7,4},{8,9},{9,10},{10,1... | collective-permute-start | bytes 61448 | tf_op jit(solution)/shard_map/ppermute | solution.py:37
  88.9 1.6 %collective-permute-start.8 = (bf16[32,8,600]{2,1,0:T(8,128)(2,1)S(1)}, bf16[32,8,600]{2,1,0:T(8,128)(2,1)S(1)}, u32[]{:S(2)}, u32[]{:S(2)}) collective-permute-start(bf16[32,8,600]{2,1,0:T(8,128)(2,1)S(1)} %all_to_all.22), channel_id=1, source_target_pairs={{0,4},{4,0},{8,12},{12,8},{16,20},{20,16},{24,28},{28,24},{32,36},... | collective-permute-start | bytes 921608 | tf_op jit(solution)/shard_map/ppermute | solution.py:26
  96.0 2.2 %collective-permute-start.9 = (f32[1280,128]{1,0:T(8,128)S(1)}, f32[1280,128]{1,0:T(8,128)S(1)}, u32[]{:S(2)}, u32[]{:S(2)}) collective-permute-start(f32[1280,128]{1,0:T(8,128)S(1)} %get-tuple-element.21), channel_id=1, source_target_pairs={{0,4},{4,0},{8,12},{12,8},{16,20},{20,16},{24,28},{28,24},{32,36},... | collective-permute-start | bytes 1966088 | tf_op jit(solution)/shard_map/ppermute | solution.py:26
  116.2 3.9 %collective-permute-start.12 = (f32[40,128]{1,0:T(8,128)S(1)}, f32[40,128]{1,0:T(8,128)S(1)}, u32[]{:S(2)}, u32[]{:S(2)}) collective-permute-start(f32[40,128]{1,0:T(8,128)S(1)} %convert_reduce_fusion.refs_0_), channel_id=1, source_target_pairs={{0,3},{1,0},{2,1},{3,2},{4,7},{5,4},{6,5},{7,6},{8,11},{9,8},{10,9... | collective-permute-start | bytes 61448 | tf_op jit(solution)/shard_map/ppermute | solution.py:37
  116.4 5.3 %collective-permute-start.11 = (f32[40,128]{1,0:T(8,128)S(1)}, f32[40,128]{1,0:T(8,128)S(1)}, u32[]{:S(2)}, u32[]{:S(2)}) collective-permute-start(f32[40,128]{1,0:T(8,128)S(1)} %convert_reduce_fusion.refs_0_), channel_id=1, source_target_pairs={{0,2},{1,3},{2,0},{3,1},{4,6},{5,7},{6,4},{7,5},{8,10},{9,11},{10,... | collective-permute-start | bytes 61448 | tf_op jit(solution)/shard_map/ppermute | solution.py:37
  117.6 5.1 %collective-permute-start.10 = (f32[40,128]{1,0:T(8,128)S(1)}, f32[40,128]{1,0:T(8,128)S(1)}, u32[]{:S(2)}, u32[]{:S(2)}) collective-permute-start(f32[40,128]{1,0:T(8,128)S(1)} %convert_reduce_fusion.refs_0_), channel_id=1, source_target_pairs={{0,1},{1,2},{2,3},{3,0},{4,5},{5,6},{6,7},{7,4},{8,9},{9,10},{10,1... | collective-permute-start | bytes 61448 | tf_op jit(solution)/shard_map/ppermute | solution.py:37

commit v2 on v1

--- a/solution.py
+++ b/solution.py
@@ -2,6 +2,7 @@
 
 import jax
 import jax.numpy as jnp
+import numpy as np
 from jax import lax
 from jax.experimental import pallas as pl
 from jax.experimental.pallas import tpu as pltpu
@@ -18,7 +19,10 @@
 
 
 def one_core_groups(count):
-    return [list(range(core, count, 2)) for core in range(2)]
+    size = count // 2
+    tall = 8
+    order = [(place % (size // tall)) * tall + place // (size // tall) for place in range(size)]
+    return [[2 * chip + core for chip in order] for core in range(2)]
 
 
 def from_other_core(value):
@@ -40,20 +44,19 @@
     return (value, *others)
 
 
-def true_id(place, each):
-    length = lax.axis_size("freq")
-    slot = (lax.axis_index("freq") + length - place // each) % length
-    return slot * each + place % each
-
-
-def phase_table(freq_ids, time_ids, part):
-    phase_int = freq_ids * time_ids % PERIOD
-    phase = phase_int.astype(jnp.float32) * (2.0 * math.pi / PERIOD)
-    return jnp.where(part == 0, jnp.cos(phase), -jnp.sin(phase))
-
-
-def iota(shape, dim):
-    return lax.broadcasted_iota(jnp.int32, shape, dim)
+def transforms(length, each_freq, each_time):
+    to_freq, to_time = [], []
+    for mine in range(length):
+        slots = (mine - np.arange(length)) % length
+        freqs = (slots[:, None] * each_freq + np.arange(each_freq)).reshape(-1)
+        times = (slots[:, None] * each_time + np.arange(each_time)).reshape(-1)
+        phase = (freqs[:, None] * times[None, :] % PERIOD).astype(np.float32)
+        phase = (phase * np.float32(2.0 * math.pi / PERIOD)).astype(np.float64)
+        both = np.stack([np.cos(phase), -np.sin(phase)]).astype(np.float32)
+        to_freq.append(both[:, :each_freq].reshape(2 * each_freq, -1))
+        both = both.reshape(2, length, each_freq, -1).transpose(1, 0, 2, 3)
+        to_time.append(both.reshape(2 * length * each_freq, -1).T)
+    return np.stack(to_freq), np.stack(to_time)
 
 
 def dot_f32(left, right):
@@ -64,18 +67,18 @@
     return jnp.sum(jnp.sum(value, axis=0, keepdims=True), axis=1, keepdims=True)
 
 
-def send_spectra(to_freq_ref, direction, out_ref):
-    spectra = dot_f32(to_freq_ref[...], direction).astype(jnp.bfloat16)
+def send_spectra(mine_ref, to_freq_ref, direction, out_ref):
+    spectra = dot_f32(to_freq_ref[mine_ref[0]], direction).astype(jnp.bfloat16)
     out_ref[...] = jnp.broadcast_to(spectra[None], out_ref.shape)
 
 
-def first_kernel(_, to_freq_ref, *refs):
+def first_kernel(_, mine_ref, to_freq_ref, *refs):
     *slots, out_ref = refs
     observed = jnp.concatenate([slot[...] for slot in slots], axis=0)
-    send_spectra(to_freq_ref, observed, out_ref)
-
-
-def applied_of(to_time_ref, noise_ref, direction, images):
+    send_spectra(mine_ref, to_freq_ref, observed, out_ref)
+
+
+def applied_of(mine_ref, to_time_ref, noise_ref, direction, images):
     sensors = direction.shape[1]
     tiles = -(-sensors // LANES)
     each = images[0].shape[0] // tiles
@@ -86,20 +89,20 @@
         ],
         axis=0,
     )[:, :sensors]
-    return noise_ref[...] * direction + dot_f32(to_time_ref[...], image)
-
-
-def middle_kernel(slots, to_freq_ref, to_time_ref, noise_ref, *refs):
+    return noise_ref[...][None, :] * direction + dot_f32(to_time_ref[mine_ref[0]], image)
+
+
+def middle_kernel(slots, mine_ref, to_freq_ref, to_time_ref, noise_ref, *refs):
     observed_refs, image_refs = refs[:slots], refs[slots : 2 * slots]
     out_ref, solution_ref, residual_ref, direction_ref, norm_ref = refs[2 * slots :]
     observed = jnp.concatenate([slot[...] for slot in observed_refs], axis=0)
-    applied = applied_of(to_time_ref, noise_ref, observed, image_refs)
+    applied = applied_of(mine_ref, to_time_ref, noise_ref, observed, image_refs)
     norm = total(observed * observed)
     step = norm / total(observed * applied)
     residual = observed - step * applied
     fresh = total(residual * residual)
     direction = residual + (fresh / norm) * observed
-    send_spectra(to_freq_ref, direction, out_ref)
+    send_spectra(mine_ref, to_freq_ref, direction, out_ref)
     own = solution_ref.shape[0]
     solution_ref[...] = (step * observed)[:own]
     residual_ref[...] = residual[:own]
@@ -107,19 +110,18 @@
     norm_ref[...] = jnp.broadcast_to(fresh, norm_ref.shape)
 
 
-def last_kernel(to_time_ref, noise_ref, solution_ref, residual_ref, direction_ref, norm_ref, *refs):
-    *image_refs, solution_out, residual_out = refs
+def last_kernel(mine_ref, to_time_ref, noise_ref, *refs):
+    solution_ref, residual_ref, direction_ref, norm_ref, *image_refs, solution_out, residual_out = refs
     direction = direction_ref[...]
-    applied = applied_of(to_time_ref, noise_ref, direction, image_refs)
+    applied = applied_of(mine_ref, to_time_ref, noise_ref, direction, image_refs)
     step = norm_ref[:1, :1] / total(direction * applied)
     own = solution_out.shape[0]
     solution_out[...] = solution_ref[...] + step * direction[:own]
     residual_out[...] = residual_ref[...] - step * applied[:own]
 
 
-def touch_kernel(*refs):
-    out = refs[-1]
-    out[...] = jnp.zeros_like(out)
+def touch_kernel(_, out_ref):
+    out_ref[...] = jnp.zeros_like(out_ref)
 
 
 def hessian_kernel(slot_count, kernel_ref, gain_ref, own_ref, other_ref, own_out, other_out):
@@ -185,30 +187,17 @@
     block = (half, 2 * slot_count, sensors)
     image_rows = -(-sensors // LANES) * 2 * slot_count
 
-    spectral = 2 * slot_count
-    shape = (spectral, NT)
-    row = iota(shape, 0)
-    to_freq = phase_table(
-        true_id(row % slot_count, slot_count),
-        true_id(iota(shape, 1), own_times),
-        row // slot_count,
-    )
-    shape = (NT, freq_size * spectral)
-    column = iota(shape, 1)
-    to_time = phase_table(
-        true_id(column // spectral * slot_count + column % slot_count, slot_count),
-        true_id(iota(shape, 0), own_times),
-        column % spectral // slot_count,
-    )
-    noise = noise_var[None, :]
+    to_freq, to_time = transforms(freq_size, slot_count, own_times)
+    mine = lax.axis_index("freq").reshape(1)
 
     full = pl.BlockSpec(memory_space=VMEM)
+    scalar = pl.BlockSpec(memory_space=pltpu.SMEM)
 
     def vmem_call(body, outs, args, name, limit=4, cost=None):
         return pl.pallas_call(
             body,
             out_shape=[jax.ShapeDtypeStruct(shape, dtype) for shape, dtype in outs],
-            in_specs=[full] * len(args),
+            in_specs=[scalar if arg is mine else full for arg in args],
             out_specs=[full] * len(outs),
             compiler_params=pltpu.CompilerParams(vmem_limit_bytes=limit * MIB),
             cost_estimate=cost,
@@ -239,12 +228,12 @@
     touched = vmem_call(
         touch_kernel,
         [((8, 128), jnp.float32)],
-        (kernel_hat, to_freq, to_time, noise),
+        (mine,),
         "touch",
-        4,
+        1,
         pl.CostEstimate(flops=10**10, bytes_accessed=10**7, transcendentals=0),
     )[0]
-    spectra = vmem_call(first_kernel, [(block, jnp.bfloat16)], (touched, to_freq, *slots), "first")[0]
+    spectra = vmem_call(first_kernel, [(block, jnp.bfloat16)], (touched, mine, to_freq, *slots), "first")[0]
     images = hessian(spectra)
     own_shape = ((own_times, sensors), jnp.float32)
     spectra, solution, residual, direction, norm = vmem_call(
@@ -256,14 +245,14 @@
             ((NT, sensors), jnp.float32),
             ((8, 128), jnp.float32),
         ],
-        (to_freq, to_time, noise, *slots, *images),
+        (mine, to_freq, to_time, noise_var, *slots, *images),
         "middle",
     )
     images = hessian(spectra)
     solution, residual = vmem_call(
         last_kernel,
         [own_shape, own_shape],
-        (to_time, noise, solution, residual, direction, norm, *images),
+        (mine, to_time, noise_var, solution, residual, direction, norm, *images),
         "last",
     )
     return solution[None], residual[None]

time: 124 us -> 120 us (0.968)
  local copies, waits for them, and re-layouts: 5.15 us -> 0.03 us
  waiting for transfers between devices: 16.4 us -> 20 us
  blocking collectives: 77 us -> 75.2 us
    unnamed x8 -> x12, local copies, waits for them, and re-layouts: 4.46 us -> 0.03 us
    ppermute x9, waiting for transfers between devices: 9.27 us -> 12.9 us  [freq_slots(): lax.ppermute(value, 'freq', [(i, (i + d) % length) for i in range(length)])]
    all_to_all x4, blocking collectives: 77 us -> 75.2 us  [exchange(): lax.all_to_all(blocks, 'param', 0, 0, axis_index_groups=groups, tiled=True)]
  transfers between devices with their start and end apart: 13 -> 13, of which waited for: 9 -> 12; matrix products, arithmetic and copies ran while one was open for 1% -> 0% of each run, Pallas kernels for 0% -> 0%
where the time goes in v2:
time: 120 us
  blocking collectives  75.2 us (63%)
  waiting for transfers between devices  20 us (17%)
  Pallas kernels  12.5 us (10%)
  starting transfers between devices  10.8 us (9%)
    all_to_all x4, blocking collectives, exchange(): lax.all_to_all(blocks, 'param', 0, 0, axis_index_groups=groups, tiled=True)  75.2 us
    ppermute x9, waiting for transfers between devices, freq_slots(): lax.ppermute(value, 'freq', [(i, (i + d) % length) for i in range(length)])  12.9 us
    pallas_call x6, Pallas kernels, vmem_call(): pl.pallas_call(body, out_shape=[jax.ShapeDtypeStruct(shape, dtype) for sh...  12.5 us
    ppermute x9, starting transfers between devices, freq_slots(): lax.ppermute(value, 'freq', [(i, (i + d) % length) for i in range(length)])  10.4 us
    ppermute x4, waiting for transfers between devices, from_other_core(): return lax.ppermute(value, 'param', [(i, i ^ 1) for i in range(count)])  7.19 us
  transfers between devices with their start and end apart: 13, of which 12 were waited for; matrix products, arithmetic and copies ran while one was open for 0% of the time, Pallas kernels for 0%

profile of v2, /device:TPU:32, one launch (start us, length us, event | category | flops | bytes accessed | tf_op | source)
XLA Modules:
  0.0 119.6 jit_solution(2223852062940330083)
XLA Ops:
  0.6 2.8 %collective-permute-start.2 = (f32[4,600]{1,0:T(4,128)}, f32[4,600]{1,0:T(4,128)S(1)}, u32[]{:S(2)}, u32[]{:S(2)}) collective-permute-start(f32[4,600]{1,0:T(4,128)} %bitcast.14), channel_id=1, source_target_pairs={{0,3},{1,0},{2,1},{3,2},{4,7},{5,4},{6,5},{7,6},{8,11},{9,8},{10,9... | collective-permute-start | bytes 28808 | tf_op jit(solution)/shard_map/ppermute | solution.py:41
  3.5 0.8 collective-permute-start.1
  4.3 0.9 collective-permute-start
  5.2 0.0 copy-start.3
  5.2 0.0 copy-start.1
  5.2 0.0 copy-start.5
  5.2 0.0 collective-permute-done.2.refs_3_.refs_7_
  5.2 3.6 %collective-permute-done.1.refs_2_.refs_6_ = f32[4,600]{1,0:T(4,128)S(1)} collective-permute-done((f32[4,600]{1,0:T(4,128)}, f32[4,600]{1,0:T(4,128)S(1)}, u32[]{:S(2)}, u32[]{:S(2)}) %collective-permute-start.1) | collective-permute-done | bytes 9632 | tf_op jit(solution)/shard_map/ppermute | solution.py:41
  8.9 0.5 collective-permute-done.refs_1_.refs_5_
  9.4 0.0 copy-done.3
  9.4 0.0 copy-done.4
  9.4 0.2 first.1
  9.6 22.8 %all_to_all.20 = bf16[32,8,600]{2,1,0:T(8,128)(2,1)S(1)} all-to-all(bf16[32,8,600]{2,1,0:T(8,128)(2,1)S(1)} %first.1), channel_id=1, replica_groups={{0,64,128,192,8,72,136,200,16,80,144,208,24,88,152,216,32,96,160,224,40..., dimensions={0} | all-to-all | bytes 614400 | tf_op jit(solution)/shard_map/all_to_all | solution.py:35
  32.4 0.0 collective-permute-start.3
  32.4 1.6 %collective-permute-done.3 = bf16[32,8,600]{2,1,0:T(8,128)(2,1)S(1)} collective-permute-done((bf16[32,8,600]{2,1,0:T(8,128)(2,1)S(1)}, bf16[32,8,600]{2,1,0:T(8,128)(2,1)S(1)}, u32[]{:S(2)}, u32[]{:S(2)}) %collective-permute-start.3) | collective-permute-done | bytes 307232 | tf_op jit(solution)/shard_map/ppermute | solution.py:30
  34.0 0.0 copy-done
  34.0 0.0 copy-done.2
  34.0 5.4 %hessian.2 = (f32[1280,128]{1,0:T(8,128)S(1)}, f32[1280,128]{1,0:T(8,128)S(1)}) custom-call(bf16[2,4,600,1024]{3,2,1,0:T(8,128)(2,1)S(1)} %copy-done, f32[4,1024]{1,0:T(4,128)S(1)} %copy-done.2, bf16[256,600]{1,0:T(8,128)(2,1)S(1)} %bitcast.10, bf16[256,600]{1,0:T(8,128)(2,1)S(1)} %bitcast.12), custom_call_target="tpu_custom_call" | custom-call | tf_op jit(solution)/shard_map/hessian/pallas_call | solution.py:197
  39.5 0.2 collective-permute-start.4
  39.7 2.0 %collective-permute-done.4 = f32[1280,128]{1,0:T(8,128)S(1)} collective-permute-done((f32[1280,128]{1,0:T(8,128)S(1)}, f32[1280,128]{1,0:T(8,128)S(1)}, u32[]{:S(2)}, u32[]{:S(2)}) %collective-permute-start.4) | collective-permute-done | bytes 655392 | tf_op jit(solution)/shard_map/ppermute | solution.py:30
  41.7 0.1 add_convert_fusion.1
  41.7 18.3 %all_to_all.21 = bf16[32,40,128]{2,1,0:T(8,128)(2,1)S(1)} all-to-all(bf16[32,40,128]{2,1,0:T(8,128)(2,1)S(1)} %bitcast.19), channel_id=1, replica_groups={{0,64,128,192,8,72,136,200,16,80,144,208,24,88,152,216,32,96,160,224,40..., dimensions={0} | all-to-all | bytes 655360 | tf_op jit(solution)/shard_map/all_to_all | solution.py:35
  60.0 0.1 convert_reduce_fusion.1.refs_8_
  60.1 1.1 collective-permute-start.7
  61.2 1.0 collective-permute-start.6
  62.2 0.9 collective-permute-start.5
  63.1 0.8 collective-permute-done.7.refs_11_
  63.9 2.5 %collective-permute-done.6.refs_10_ = f32[40,128]{1,0:T(8,128)S(1)} collective-permute-done((f32[40,128]{1,0:T(8,128)S(1)}, f32[40,128]{1,0:T(8,128)S(1)}, u32[]{:S(2)}, u32[]{:S(2)}) %collective-permute-start.6) | collective-permute-done | bytes 20512 | tf_op jit(solution)/shard_map/ppermute | solution.py:41
  66.5 0.7 collective-permute-done.5.refs_9_
  67.2 0.0 copy-done.1
  67.2 0.0 copy-done.5
  67.2 0.6 middle.1
  67.8 15.9 %all_to_all.22 = bf16[32,8,600]{2,1,0:T(8,128)(2,1)S(1)} all-to-all(bf16[32,8,600]{2,1,0:T(8,128)(2,1)S(1)} %get-tuple-element.19), channel_id=1, replica_groups={{0,64,128,192,8,72,136,200,16,80,144,208,24,88,152,216,32,96,160,224,40..., dimensions={0} | all-to-all | bytes 614400 | tf_op jit(solution)/shard_map/all_to_all | solution.py:35
  83.6 0.0 collective-permute-start.8
  83.6 1.6 %collective-permute-done.8 = bf16[32,8,600]{2,1,0:T(8,128)(2,1)S(1)} collective-permute-done((bf16[32,8,600]{2,1,0:T(8,128)(2,1)S(1)}, bf16[32,8,600]{2,1,0:T(8,128)(2,1)S(1)}, u32[]{:S(2)}, u32[]{:S(2)}) %collective-permute-start.8) | collective-permute-done | bytes 307232 | tf_op jit(solution)/shard_map/ppermute | solution.py:30
  85.2 5.4 %hessian.3 = (f32[1280,128]{1,0:T(8,128)S(1)}, f32[1280,128]{1,0:T(8,128)S(1)}) custom-call(bf16[2,4,600,1024]{3,2,1,0:T(8,128)(2,1)S(1)} %copy-done, f32[4,1024]{1,0:T(4,128)S(1)} %copy-done.2, bf16[256,600]{1,0:T(8,128)(2,1)S(1)} %bitcast.11, bf16[256,600]{1,0:T(8,128)(2,1)S(1)} %bitcast.13), custom_call_target="tpu_custom_call" | custom-call | tf_op jit(solution)/shard_map/hessian/pallas_call | solution.py:197
  90.7 0.2 collective-permute-start.9
  90.9 2.0 %collective-permute-done.9 = f32[1280,128]{1,0:T(8,128)S(1)} collective-permute-done((f32[1280,128]{1,0:T(8,128)S(1)}, f32[1280,128]{1,0:T(8,128)S(1)}, u32[]{:S(2)}, u32[]{:S(2)}) %collective-permute-start.9) | collective-permute-done | bytes 655392 | tf_op jit(solution)/shard_map/ppermute | solution.py:30
  92.9 0.1 add_convert_fusion
  92.9 18.2 %all_to_all.23 = bf16[32,40,128]{2,1,0:T(8,128)(2,1)S(1)} all-to-all(bf16[32,40,128]{2,1,0:T(8,128)(2,1)S(1)} %bitcast.20), channel_id=1, replica_groups={{0,64,128,192,8,72,136,200,16,80,144,208,24,88,152,216,32,96,160,224,40..., dimensions={0} | all-to-all | bytes 655360 | tf_op jit(solution)/shard_map/all_to_all | solution.py:35
  111.1 0.1 convert_reduce_fusion.refs_4_
  111.2 1.8 %collective-permute-start.12 = (f32[40,128]{1,0:T(8,128)S(1)}, f32[40,128]{1,0:T(8,128)S(1)}, u32[]{:S(2)}, u32[]{:S(2)}) collective-permute-start(f32[40,128]{1,0:T(8,128)S(1)} %convert_reduce_fusion.refs_4_), channel_id=1, source_target_pairs={{0,3},{1,0},{2,1},{3,2},{4,7},{5,4},{6,5},{7,6},{8,11},{9,8},{10,9... | collective-permute-start | bytes 61448 | tf_op jit(solution)/shard_map/ppermute | solution.py:41
  113.0 0.7 collective-permute-start.11
  113.7 0.3 collective-permute-start.10
  114.0 1.0 collective-permute-done.12.refs_7_
  115.1 3.2 %collective-permute-done.11.refs_6_ = f32[40,128]{1,0:T(8,128)S(1)} collective-permute-done((f32[40,128]{1,0:T(8,128)S(1)}, f32[40,128]{1,0:T(8,128)S(1)}, u32[]{:S(2)}, u32[]{:S(2)}) %collective-permute-start.11) | collective-permute-done | bytes 20512 | tf_op jit(solution)/shard_map/ppermute | solution.py:41
  118.3 0.4 collective-permute-done.10.refs_5_
  118.7 0.9 last.1
  (4 shorter events, 0.0 us)
Async XLA Ops:
  0.6 4.6 %collective-permute-start.2 = (f32[4,600]{1,0:T(4,128)}, f32[4,600]{1,0:T(4,128)S(1)}, u32[]{:S(2)}, u32[]{:S(2)}) collective-permute-start(f32[4,600]{1,0:T(4,128)} %bitcast.14), channel_id=1, source_target_pairs={{0,3},{1,0},{2,1},{3,2},{4,7},{5,4},{6,5},{7,6},{8,11},{9,8},{10,9... | collective-permute-start | bytes 28808 | tf_op jit(solution)/shard_map/ppermute | solution.py:41
  3.5 5.4 %collective-permute-start.1 = (f32[4,600]{1,0:T(4,128)}, f32[4,600]{1,0:T(4,128)S(1)}, u32[]{:S(2)}, u32[]{:S(2)}) collective-permute-start(f32[4,600]{1,0:T(4,128)} %bitcast.15), channel_id=1, source_target_pairs={{0,2},{1,3},{2,0},{3,1},{4,6},{5,7},{6,4},{7,5},{8,10},{9,11},{10,... | collective-permute-start | bytes 28808 | tf_op jit(solution)/shard_map/ppermute | solution.py:41
  4.3 5.1 %collective-permute-start = (f32[4,600]{1,0:T(4,128)}, f32[4,600]{1,0:T(4,128)S(1)}, u32[]{:S(2)}, u32[]{:S(2)}) collective-permute-start(f32[4,600]{1,0:T(4,128)} %bitcast.16), channel_id=1, source_target_pairs={{0,1},{1,2},{2,3},{3,0},{4,5},{5,6},{6,7},{7,4},{8,9},{9,10},{10,1... | collective-permute-start | bytes 28808 | tf_op jit(solution)/shard_map/ppermute | solution.py:41
  5.2 4.2 %copy-start.3 = (f32[4,8,16]{2,1,0:T(8,128)S(1)}, f32[4,8,16]{2,1,0:T(8,128)}, u32[]{:S(2)}) copy-start(f32[4,8,16]{2,1,0:T(8,128)} %constant.10.clone.to_freq_ref.refs_1_) | copy-start | bytes 6148
  5.2 4.2 %copy-start.4 = (f32[1,4,600]{2,1,0:T(4,128)S(1)}, f32[1,4,600]{2,1,0:T(4,128)}, u32[]{:S(2)}) copy-start(f32[1,4,600]{2,1,0:T(4,128)} %param.9) | copy-start | bytes 28804
  5.2 28.9 %copy-start = (bf16[2,4,600,1024]{3,2,1,0:T(8,128)(2,1)S(1)}, bf16[2,4,600,1024]{3,2,1,0:T(8,128)(2,1)}, u32[]{:S(2)}) copy-start(bf16[2,4,600,1024]{3,2,1,0:T(8,128)(2,1)} %refs_0_.3) | copy-start | bytes 29491204
  5.2 28.9 %copy-start.2 = (f32[4,1024]{1,0:T(4,128)S(1)}, f32[4,1024]{1,0:T(4,128)}, u32[]{:S(2)}) copy-start(f32[4,1024]{1,0:T(4,128)} %refs_1_.4) | copy-start | bytes 49156
  5.2 62.0 %copy-start.1 = (f32[4,16,32]{2,1,0:T(8,128)S(1)}, f32[4,16,32]{2,1,0:T(8,128)}, u32[]{:S(2)}) copy-start(f32[4,16,32]{2,1,0:T(8,128)} %constant.11.clone.refs_2_.to_time_ref) | copy-start | bytes 24580
  5.2 62.0 %copy-start.5 = (f32[600]{0:T(1024)S(1)}, f32[600]{0:T(1024)}, u32[]{:S(2)}) copy-start(f32[600]{0:T(1024)} %noise_ref.1) | copy-start | bytes 7204
  32.4 1.6 %collective-permute-start.3 = (bf16[32,8,600]{2,1,0:T(8,128)(2,1)S(1)}, bf16[32,8,600]{2,1,0:T(8,128)(2,1)S(1)}, u32[]{:S(2)}, u32[]{:S(2)}) collective-permute-start(bf16[32,8,600]{2,1,0:T(8,128)(2,1)S(1)} %all_to_all.20), channel_id=1, source_target_pairs={{0,4},{4,0},{8,12},{12,8},{16,20},{20,16},{24,28},{28,24},{32,36},... | collective-permute-start | bytes 921608 | tf_op jit(solution)/shard_map/ppermute | solution.py:30
  39.5 2.2 %collective-permute-start.4 = (f32[1280,128]{1,0:T(8,128)S(1)}, f32[1280,128]{1,0:T(8,128)S(1)}, u32[]{:S(2)}, u32[]{:S(2)}) collective-permute-start(f32[1280,128]{1,0:T(8,128)S(1)} %get-tuple-element.14), channel_id=1, source_target_pairs={{0,4},{4,0},{8,12},{12,8},{16,20},{20,16},{24,28},{28,24},{32,36},... | collective-permute-start | bytes 1966088 | tf_op jit(solution)/shard_map/ppermute | solution.py:30
  60.1 3.9 %collective-permute-start.7 = (f32[40,128]{1,0:T(8,128)S(1)}, f32[40,128]{1,0:T(8,128)S(1)}, u32[]{:S(2)}, u32[]{:S(2)}) collective-permute-start(f32[40,128]{1,0:T(8,128)S(1)} %convert_reduce_fusion.1.refs_8_), channel_id=1, source_target_pairs={{0,3},{1,0},{2,1},{3,2},{4,7},{5,4},{6,5},{7,6},{8,11},{9,8},{10,9... | collective-permute-start | bytes 61448 | tf_op jit(solution)/shard_map/ppermute | solution.py:41
  61.2 5.3 %collective-permute-start.6 = (f32[40,128]{1,0:T(8,128)S(1)}, f32[40,128]{1,0:T(8,128)S(1)}, u32[]{:S(2)}, u32[]{:S(2)}) collective-permute-start(f32[40,128]{1,0:T(8,128)S(1)} %convert_reduce_fusion.1.refs_8_), channel_id=1, source_target_pairs={{0,2},{1,3},{2,0},{3,1},{4,6},{5,7},{6,4},{7,5},{8,10},{9,11},{10,... | collective-permute-start | bytes 61448 | tf_op jit(solution)/shard_map/ppermute | solution.py:41
  62.2 5.0 %collective-permute-start.5 = (f32[40,128]{1,0:T(8,128)S(1)}, f32[40,128]{1,0:T(8,128)S(1)}, u32[]{:S(2)}, u32[]{:S(2)}) collective-permute-start(f32[40,128]{1,0:T(8,128)S(1)} %convert_reduce_fusion.1.refs_8_), channel_id=1, source_target_pairs={{0,1},{1,2},{2,3},{3,0},{4,5},{5,6},{6,7},{7,4},{8,9},{9,10},{10,1... | collective-permute-start | bytes 61448 | tf_op jit(solution)/shard_map/ppermute | solution.py:41
  83.6 1.6 %collective-permute-start.8 = (bf16[32,8,600]{2,1,0:T(8,128)(2,1)S(1)}, bf16[32,8,600]{2,1,0:T(8,128)(2,1)S(1)}, u32[]{:S(2)}, u32[]{:S(2)}) collective-permute-start(bf16[32,8,600]{2,1,0:T(8,128)(2,1)S(1)} %all_to_all.22), channel_id=1, source_target_pairs={{0,4},{4,0},{8,12},{12,8},{16,20},{20,16},{24,28},{28,24},{32,36},... | collective-permute-start | bytes 921608 | tf_op jit(solution)/shard_map/ppermute | solution.py:30
  90.7 2.2 %collective-permute-start.9 = (f32[1280,128]{1,0:T(8,128)S(1)}, f32[1280,128]{1,0:T(8,128)S(1)}, u32[]{:S(2)}, u32[]{:S(2)}) collective-permute-start(f32[1280,128]{1,0:T(8,128)S(1)} %get-tuple-element.21), channel_id=1, source_target_pairs={{0,4},{4,0},{8,12},{12,8},{16,20},{20,16},{24,28},{28,24},{32,36},... | collective-permute-start | bytes 1966088 | tf_op jit(solution)/shard_map/ppermute | solution.py:30
  111.2 3.9 %collective-permute-start.12 = (f32[40,128]{1,0:T(8,128)S(1)}, f32[40,128]{1,0:T(8,128)S(1)}, u32[]{:S(2)}, u32[]{:S(2)}) collective-permute-start(f32[40,128]{1,0:T(8,128)S(1)} %convert_reduce_fusion.refs_4_), channel_id=1, source_target_pairs={{0,3},{1,0},{2,1},{3,2},{4,7},{5,4},{6,5},{7,6},{8,11},{9,8},{10,9... | collective-permute-start | bytes 61448 | tf_op jit(solution)/shard_map/ppermute | solution.py:41
  113.0 5.3 %collective-permute-start.11 = (f32[40,128]{1,0:T(8,128)S(1)}, f32[40,128]{1,0:T(8,128)S(1)}, u32[]{:S(2)}, u32[]{:S(2)}) collective-permute-start(f32[40,128]{1,0:T(8,128)S(1)} %convert_reduce_fusion.refs_4_), channel_id=1, source_target_pairs={{0,2},{1,3},{2,0},{3,1},{4,6},{5,7},{6,4},{7,5},{8,10},{9,11},{10,... | collective-permute-start | bytes 61448 | tf_op jit(solution)/shard_map/ppermute | solution.py:41
  113.7 5.0 %collective-permute-start.10 = (f32[40,128]{1,0:T(8,128)S(1)}, f32[40,128]{1,0:T(8,128)S(1)}, u32[]{:S(2)}, u32[]{:S(2)}) collective-permute-start(f32[40,128]{1,0:T(8,128)S(1)} %convert_reduce_fusion.refs_4_), channel_id=1, source_target_pairs={{0,1},{1,2},{2,3},{3,0},{4,5},{5,6},{6,7},{7,4},{8,9},{9,10},{10,1... | collective-permute-start | bytes 61448 | tf_op jit(solution)/shard_map/ppermute | solution.py:41

commit v3 on v2

v3 whole, which is shorter than its diff:
```python
import math

import jax
import jax.numpy as jnp
import numpy as np
from jax import lax
from jax.experimental import pallas as pl
from jax.experimental.pallas import tpu as pltpu
from jax.sharding import PartitionSpec as P

NT = 16
ITERS = 2
PERIOD = 2 * NT - 1

HIGHEST = lax.Precision.HIGHEST
VMEM = pltpu.VMEM
LANES = 128
MIB = 1024 * 1024


def one_core_groups(count):
    size = count // 2
    tall = 8
    order = [(place % (size // tall)) * tall + place // (size // tall) for place in range(size)]
    return [[2 * chip + core for chip in order] for core in range(2)]


def from_other_core(value):
    count = lax.axis_size("param")
    return lax.ppermute(value, "param", [(i, i ^ 1) for i in range(count)])


def exchange(blocks):
    groups = one_core_groups(lax.axis_size("param"))
    return lax.all_to_all(blocks, "param", 0, 0, axis_index_groups=groups, tiled=True)


def freq_slots(value):
    length = lax.axis_size("freq")
    others = [
        lax.ppermute(value, "freq", [(i, (i + d) % length) for i in range(length)])
        for d in range(1, length)
    ]
    return (value, *others)


def transforms(length, slot_count, own_times):
    each = slot_count // 2
    sides = np.arange(2)

    def table(freqs, times):
        phase = (freqs * times % PERIOD).astype(np.float32)
        phase = (phase * np.float32(2.0 * math.pi / PERIOD)).astype(np.float64)
        return np.stack([np.cos(phase), -np.sin(phase)]).astype(np.float32)

    to_freq = np.zeros((length, 2, 2, 2, each, length, 2, own_times), np.float32)
    to_time = np.zeros((length, 2, length, 2, own_times, length, 2, 2, 2, each), np.float32)
    for mine in range(length):
        slots = (mine - np.arange(length)) % length
        times = slots[:, None] * own_times + np.arange(own_times)
        for core in range(2):
            freqs = mine * slot_count + core * each + np.arange(each)
            values = table(freqs[:, None, None], times)
            for side in sides:
                to_freq[mine, core, side, :, :, :, side] = values
            for source in sides:
                first = slots * slot_count + (core + source) % 2 * each
                freqs = first[:, None] + np.arange(each)
                values = table(freqs, times[:, :, None, None]).transpose(1, 2, 3, 0, 4)
                for side in sides:
                    to_time[mine, core, :, side, :, :, source, (side + source) % 2] = values
    rows = 4 * each
    times = 2 * length * own_times
    return (
        to_freq.reshape(length, 2, rows, times),
        to_time.reshape(length, 2, times, 2 * length * rows),
    )


def dot_f32(left, right):
    return jnp.dot(left, right, precision=HIGHEST, preferred_element_type=jnp.float32)


def side_sums(value, own_times):
    rows = jnp.sum(value, axis=1, keepdims=True)
    own = lax.broadcasted_iota(jnp.int32, rows.shape, 0) // own_times % 2 == 0
    sums = [
        jnp.sum(jnp.where(keep, rows, 0.0), axis=0, keepdims=True)
        for keep in (own, jnp.logical_not(own))
    ]
    return jnp.where(own, *sums)


def send_spectra(mine_ref, core_ref, to_freq_ref, direction, out_ref):
    spectra = dot_f32(to_freq_ref[mine_ref[0], core_ref[0]], direction).astype(jnp.bfloat16)
    out_ref[...] = jnp.broadcast_to(spectra[None], out_ref.shape)


def first_kernel(_, mine_ref, core_ref, to_freq_ref, *refs):
    *slots, out_ref = refs
    observed = jnp.concatenate([slot[...] for slot in slots], axis=0)
    send_spectra(mine_ref, core_ref, to_freq_ref, observed, out_ref)


def applied_of(mine_ref, core_ref, to_time_ref, noise_ref, direction, images):
    sensors = direction.shape[1]
    tiles = -(-sensors // LANES)
    rows = to_time_ref.shape[-1] // (2 * len(images))
    image = jnp.concatenate(
        [
            jnp.concatenate(
                [slot[start + i * rows : start + (i + 1) * rows] for i in range(tiles)], axis=1
            )
            for slot in images
            for start in (0, tiles * rows)
        ],
        axis=0,
    )[:, :sensors]
    inverse = dot_f32(to_time_ref[mine_ref[0], core_ref[0]], image)
    return noise_ref[...][None, :] * direction + inverse


def middle_kernel(slots, mine_ref, core_ref, to_freq_ref, to_time_ref, noise_ref, *refs):
    observed_refs, image_refs = refs[:slots], refs[slots : 2 * slots]
    out_ref, solution_ref, residual_ref, direction_ref, norm_ref = refs[2 * slots :]
    own = solution_ref.shape[0]
    observed = jnp.concatenate([slot[...] for slot in observed_refs], axis=0)
    applied = applied_of(mine_ref, core_ref, to_time_ref, noise_ref, observed, image_refs)
    norm = side_sums(observed * observed, own)
    step = norm / side_sums(observed * applied, own)
    residual = observed - step * applied
    fresh = side_sums(residual * residual, own)
    direction = residual + (fresh / norm) * observed
    send_spectra(mine_ref, core_ref, to_freq_ref, direction, out_ref)
    solution_ref[...] = (step * observed)[:own]
    residual_ref[...] = residual[:own]
    direction_ref[...] = direction
    norm_ref[...] = jnp.broadcast_to(fresh[:8], norm_ref.shape)


def last_kernel(mine_ref, core_ref, to_time_ref, noise_ref, *refs):
    solution_ref, residual_ref, direction_ref, norm_ref, *image_refs = refs[:-2]
    solution_out, residual_out = refs[-2:]
    own = solution_out.shape[0]
    direction = direction_ref[...]
    applied = applied_of(mine_ref, core_ref, to_time_ref, noise_ref, direction, image_refs)
    step = norm_ref[:1, :1] / side_sums(direction * applied, own)[:1]
    solution_out[...] = solution_ref[...] + step * direction[:own]
    residual_out[...] = residual_ref[...] - step * applied[:own]


def touch_kernel(*refs):
    out_ref = refs[-1]
    out_ref[...] = jnp.zeros_like(out_ref)


def hessian_kernel(core_ref, *refs):
    own_kernel, other_kernel, own_gain, other_gain, spectra_ref, out_ref = refs
    rows, sensors = spectra_ref.shape
    each = own_kernel.shape[1] // 2
    block = 4 * each
    half = rows // block
    tiles = -(-sensors // LANES)
    spare = jnp.zeros((half, tiles * LANES - sensors), jnp.float32)
    row = lax.broadcasted_iota(jnp.int32, (rows, rows), 0)
    column = lax.broadcasted_iota(jnp.int32, (rows, rows), 1)
    wanted = row % half * block + row // half % 4 * each + row // (4 * half)
    pick = (column == wanted).astype(jnp.float32).astype(jnp.bfloat16)
    picked = jnp.dot(pick, spectra_ref[...], preferred_element_type=jnp.float32)
    picked = picked.astype(jnp.bfloat16)
    contract = (((1,), (1,)), ((), ()))
    base = core_ref[0] * each

    def both_cores(part, slot):
        at = base + slot
        return jnp.concatenate([own_kernel[part, at], other_kernel[part, at]], axis=1)

    def forward(slot):
        spectra = picked[slot * 4 * half : (slot + 1) * 4 * half]
        by_real, by_imag = [
            jnp.dot(spectra, both_cores(part, slot), preferred_element_type=jnp.float32)
            for part in range(2)
        ]
        gain = jnp.concatenate(
            [ref[pl.ds(base + slot, 1), :] for ref in (own_gain, other_gain)], axis=1
        )
        coeffs = []
        for at in (0, 2 * half):
            upper, lower = slice(at, at + half), slice(at + half, at + 2 * half)
            coeffs.append(((by_real[upper] + by_imag[lower]) * gain).astype(jnp.bfloat16))
            coeffs.append(((by_real[lower] - by_imag[upper]) * gain).astype(jnp.bfloat16))
        return jnp.concatenate(coeffs, axis=0)

    def backward(slot, coeffs):
        by_real, by_imag = [
            lax.dot_general(
                coeffs, both_cores(part, slot), contract, preferred_element_type=jnp.float32
            )
            for part in range(2)
        ]
        for side in range(2):
            upper = slice(2 * side * half, (2 * side + 1) * half)
            lower = slice((2 * side + 1) * half, (2 * side + 2) * half)
            images = (by_real[upper] - by_imag[lower], by_real[lower] + by_imag[upper])
            for part, image in enumerate(images):
                image = jnp.concatenate([image, spare], axis=1)
                for tile in range(tiles):
                    start = tile * block + (2 * side + part) * each + slot
                    out_ref[pl.ds(start, half, stride=block * tiles), :] = image[
                        :, tile * LANES : (tile + 1) * LANES
                    ]

    coeffs = forward(0)
    for slot in range(each):
        following = forward(slot + 1) if slot + 1 < each else None
        backward(slot, coeffs)
        coeffs = following


def local(kernel_hat, prior_gain, noise_var, observed):
    slot_count, sensors, params = kernel_hat.shape[1:]
    own_times = observed.shape[1]
    freq_size = lax.axis_size("freq")
    half = lax.axis_size("param") // 2
    block = 2 * slot_count
    rows = half * block
    times = 2 * freq_size * own_times
    image_rows = -(-sensors // LANES) * block
    to_freq, to_time = transforms(freq_size, slot_count, own_times)
    mine = lax.axis_index("freq").reshape(1)
    core = (lax.axis_index("param") & 1).reshape(1)

    full = pl.BlockSpec(memory_space=VMEM)
    scalar = pl.BlockSpec(memory_space=pltpu.SMEM)

    def vmem_call(body, outs, args, name, limit=4, cost=None):
        return pl.pallas_call(
            body,
            out_shape=[jax.ShapeDtypeStruct(shape, dtype) for shape, dtype in outs],
            in_specs=[scalar if arg is mine or arg is core else full for arg in args],
            out_specs=[full] * len(outs),
            compiler_params=pltpu.CompilerParams(vmem_limit_bytes=limit * MIB),
            cost_estimate=cost,
            name=name,
        )(*args)

    def with_other_core(value):
        return jnp.concatenate([value, from_other_core(value)], axis=0)

    other_gain = from_other_core(prior_gain)
    slots = freq_slots(with_other_core(observed[0]))
    touched = vmem_call(
        touch_kernel,
        [((8, 128), jnp.float32)],
        (mine, core),
        "touch",
        1,
        pl.CostEstimate(flops=10**10, bytes_accessed=10**7, transcendentals=0),
    )[0]
    ahead = (kernel_hat, slots[0], other_gain, mine, core)
    other_kernel = from_other_core(lax.optimization_barrier(ahead)[0])

    def hessian(spectra):
        image = vmem_call(
            hessian_kernel,
            [((half * image_rows, LANES), jnp.float32)],
            (
                core,
                kernel_hat,
                other_kernel,
                prior_gain,
                other_gain,
                exchange(spectra).reshape(rows, sensors),
            ),
            "hessian",
            16,
        )[0]
        sent = image.astype(jnp.bfloat16).reshape(half, image_rows, LANES)
        return freq_slots(with_other_core(exchange(sent).astype(jnp.float32).sum(axis=0)))

    ahead = (half, block, sensors)
    spectra = vmem_call(
        first_kernel,
        [(ahead, jnp.bfloat16)],
        (touched, mine, core, to_freq, *slots),
        "first",
    )[0]
    images = hessian(spectra)
    own_shape = ((own_times, sensors), jnp.float32)
    spectra, solution, residual, direction, norm = vmem_call(
        lambda *refs: middle_kernel(freq_size, *refs),
        [
            (ahead, jnp.bfloat16),
            own_shape,
            own_shape,
            ((times, sensors), jnp.float32),
            ((8, 128), jnp.float32),
        ],
        (mine, core, to_freq, to_time, noise_var, *slots, *images),
        "middle",
    )
    images = hessian(spectra)
    solution, residual = vmem_call(
        last_kernel,
        [own_shape, own_shape],
        (mine, core, to_time, noise_var, solution, residual, direction, norm, *images),
        "last",
    )
    return solution[None], residual[None]


def solution(mesh):
    return jax.shard_map(
        local,
        mesh=mesh,
        in_specs=(
            P(None, "freq", None, "param"),
            P("freq", "param"),
            P(),
            P("param", "freq", None),
        ),
        out_specs=(P("param", "freq", None), P("param", "freq", None)),
        check_vma=False,
    )
```

time: 120 us -> 117 us (0.975)
  waiting for transfers between devices: 20 us -> 16.4 us
  blocking collectives: 75.2 us -> 73.1 us
  starting transfers between devices: 10.8 us -> 12.2 us
    ppermute x4 -> x5, waiting for transfers between devices: 7.19 us -> 3.23 us  [from_other_core(): return lax.ppermute(value, 'param', [(i, i ^ 1) for i in range(count)])]
    all_to_all x4, blocking collectives: 75.2 us -> 73.1 us  [exchange(): lax.all_to_all(blocks, 'param', 0, 0, axis_index_groups=groups, tiled=True)]
  transfers between devices with their start and end apart: 13 -> 14, of which waited for: 12 -> 11; matrix products, arithmetic and copies ran while one was open for 0% -> 1% of each run, Pallas kernels for 0% -> 0%
where the time goes in v3:
time: 117 us; the launch traced here: 116 us
  blocking collectives  73.1 us (62%)
  waiting for transfers between devices  16.4 us (14%)
  starting transfers between devices  12.2 us (10%)
  Pallas kernels  12 us (10%)
    all_to_all x4, blocking collectives, exchange(): lax.all_to_all(blocks, 'param', 0, 0, axis_index_groups=groups, tiled=True)  73.1 us
    ppermute x9, waiting for transfers between devices, freq_slots(): lax.ppermute(value, 'freq', [(i, (i + d) % length) for i in range(length)])  13.2 us
    pallas_call x6, Pallas kernels, vmem_call(): pl.pallas_call(body, out_shape=[jax.ShapeDtypeStruct(shape, dtype) for sh...  12 us
    ppermute x9, starting transfers between devices, freq_slots(): lax.ppermute(value, 'freq', [(i, (i + d) % length) for i in range(length)])  11.2 us
    ppermute x5, waiting for transfers between devices, from_other_core(): return lax.ppermute(value, 'param', [(i, i ^ 1) for i in range(count)])  3.23 us
  transfers between devices with their start and end apart: 14, of which 11 were waited for; matrix products, arithmetic and copies ran while one was open for 1% of the time, Pallas kernels for 0%

profile of v3, /device:TPU:32, one launch (start us, length us, event | category | flops | bytes accessed | tf_op | source)
XLA Modules:
  0.0 115.5 jit_solution(18281900093421783112)
XLA Ops:
  0.6 0.1 collective-permute-start
  0.7 0.5 collective-permute-start.4
  1.2 0.9 collective-permute-done
  2.1 0.7 pad_maximum_fusion.2.refs_0_.refs_5_
  2.8 0.0 collective-permute-done.4.refs_3_
  2.8 0.0 slice-start
  2.8 0.0 copy-start.1
  2.8 0.0 slice-start.1
  2.9 0.0 slice-start.2
  2.9 0.0 copy-start.2
  2.9 0.3 collective-permute-start.5
  3.1 2.8 %collective-permute-start.3 = (f32[8,600]{1,0:T(8,128)S(1)}, f32[8,600]{1,0:T(8,128)S(1)}, u32[]{:S(2)}, u32[]{:S(2)}) collective-permute-start(f32[8,600]{1,0:T(8,128)S(1)} %pad_maximum_fusion.2.refs_0_.refs_5_), channel_id=1, source_target_pairs={{0,3},{1,0},{2,1},{3,2},{4,7},{5,4},{6,5},{7,6},{8,11},{9,8},{10,9... | collective-permute-start | bytes 57608 | tf_op jit(solution)/shard_map/ppermute | solution.py:41
  5.9 0.8 collective-permute-start.2
  6.7 0.9 collective-permute-start.1
  7.6 0.0 collective-permute-done.3.refs_3_.refs_8_
  7.6 3.6 %collective-permute-done.2.refs_2_.refs_7_ = f32[8,600]{1,0:T(8,128)S(1)} collective-permute-done((f32[8,600]{1,0:T(8,128)S(1)}, f32[8,600]{1,0:T(8,128)S(1)}, u32[]{:S(2)}, u32[]{:S(2)}) %collective-permute-start.2) | collective-permute-done | bytes 19232 | tf_op jit(solution)/shard_map/ppermute | solution.py:41
  11.2 0.5 collective-permute-done.1.refs_1_.refs_6_
  11.7 0.2 first.1
  11.9 23.4 %all_to_all.20 = bf16[32,8,600]{2,1,0:T(8,128)(2,1)S(1)} all-to-all(bf16[32,8,600]{2,1,0:T(8,128)(2,1)S(1)} %first.1), channel_id=1, replica_groups={{0,64,128,192,8,72,136,200,16,80,144,208,24,88,152,216,32,96,160,224,40..., dimensions={0} | all-to-all | bytes 614400 | tf_op jit(solution)/shard_map/all_to_all | solution.py:35
  35.3 0.0 collective-permute-done.5.refs_1_
  35.3 0.0 copy-start
  35.3 0.0 copy-start.3
  35.3 5.1 %hessian.2 = f32[1280,128]{1,0:T(8,128)S(1)} custom-call(s32[1]{0:T(128)} %bitcast.1.refs_1_.core_ref, bf16[2,4,600,1024]{3,2,1,0:T(8,128)(2,1)S(1)} %bitcast.10, bf16[2,4,600,1024]{3,2,1,0:T(8,128)(2,1)S(1)} %collective-permute-done.5.refs_1_, f32[4,1024]{1,0:T(4,128)S(1)} %copy-done.2, f32[4,1024]{1,0:T(4,128)S(1)} %collective-permute-done.4.refs_3_, ...), custom_call_target="tpu_custom_call" | custom-call | tf_op jit(solution)/shard_map/hessian/pallas_call | solution.py:237
  40.5 16.7 %all_to_all.21 = bf16[32,40,128]{2,1,0:T(8,128)(2,1)S(1)} all-to-all(bf16[32,40,128]{2,1,0:T(8,128)(2,1)S(1)} %bitcast.13), channel_id=1, replica_groups={{0,64,128,192,8,72,136,200,16,80,144,208,24,88,152,216,32,96,160,224,40..., dimensions={0} | all-to-all | bytes 655360 | tf_op jit(solution)/shard_map/all_to_all | solution.py:35
  57.2 0.1 convert_reduce_fusion.1
  57.2 0.1 collective-permute-start.6
  57.3 1.2 %collective-permute-done.6 = f32[40,128]{1,0:T(8,128)S(1)} collective-permute-done((f32[40,128]{1,0:T(8,128)S(1)}, f32[40,128]{1,0:T(8,128)S(1)}, u32[]{:S(2)}, u32[]{:S(2)}) %collective-permute-start.6) | collective-permute-done | bytes 20512 | tf_op jit(solution)/shard_map/ppermute | solution.py:30
  58.5 1.2 collective-permute-start.9
  59.7 1.1 collective-permute-start.8
  60.7 1.1 collective-permute-start.7
  61.9 0.9 collective-permute-done.9.refs_12_
  62.7 2.8 %collective-permute-done.8.refs_11_ = f32[80,128]{1,0:T(8,128)S(1)} collective-permute-done((f32[80,128]{1,0:T(8,128)S(1)}, f32[80,128]{1,0:T(8,128)S(1)}, u32[]{:S(2)}, u32[]{:S(2)}) %collective-permute-start.8) | collective-permute-done | bytes 40992 | tf_op jit(solution)/shard_map/ppermute | solution.py:41
  65.5 0.5 collective-permute-done.7.refs_10_
  66.0 0.0 copy-done.3
  66.0 0.6 middle.1
  66.6 16.7 %all_to_all.22 = bf16[32,8,600]{2,1,0:T(8,128)(2,1)S(1)} all-to-all(bf16[32,8,600]{2,1,0:T(8,128)(2,1)S(1)} %get-tuple-element.15), channel_id=1, replica_groups={{0,64,128,192,8,72,136,200,16,80,144,208,24,88,152,216,32,96,160,224,40..., dimensions={0} | all-to-all | bytes 614400 | tf_op jit(solution)/shard_map/all_to_all | solution.py:35
  83.3 5.1 %hessian.3 = f32[1280,128]{1,0:T(8,128)S(1)} custom-call(s32[1]{0:T(128)} %bitcast.1.refs_1_.core_ref, bf16[2,4,600,1024]{3,2,1,0:T(8,128)(2,1)S(1)} %bitcast.10, bf16[2,4,600,1024]{3,2,1,0:T(8,128)(2,1)S(1)} %collective-permute-done.5.refs_1_, f32[4,1024]{1,0:T(4,128)S(1)} %copy-done.2, f32[4,1024]{1,0:T(4,128)S(1)} %collective-permute-done.4.refs_3_, ...), custom_call_target="tpu_custom_call" | custom-call | tf_op jit(solution)/shard_map/hessian/pallas_call | solution.py:237
  88.5 16.3 %all_to_all.23 = bf16[32,40,128]{2,1,0:T(8,128)(2,1)S(1)} all-to-all(bf16[32,40,128]{2,1,0:T(8,128)(2,1)S(1)} %bitcast.14), channel_id=1, replica_groups={{0,64,128,192,8,72,136,200,16,80,144,208,24,88,152,216,32,96,160,224,40..., dimensions={0} | all-to-all | bytes 655360 | tf_op jit(solution)/shard_map/all_to_all | solution.py:35
  104.8 0.1 convert_reduce_fusion
  104.9 0.1 collective-permute-start.10
  105.0 1.2 %collective-permute-done.10 = f32[40,128]{1,0:T(8,128)S(1)} collective-permute-done((f32[40,128]{1,0:T(8,128)S(1)}, f32[40,128]{1,0:T(8,128)S(1)}, u32[]{:S(2)}, u32[]{:S(2)}) %collective-permute-start.10) | collective-permute-done | bytes 20512 | tf_op jit(solution)/shard_map/ppermute | solution.py:30
  106.2 2.4 %collective-permute-start.13 = (f32[80,128]{1,0:T(8,128)S(1)}, f32[80,128]{1,0:T(8,128)S(1)}, u32[]{:S(2)}, u32[]{:S(2)}) collective-permute-start(f32[80,128]{1,0:T(8,128)S(1)} %pad_maximum_fusion.1.refs_4_), channel_id=1, source_target_pairs={{0,3},{1,0},{2,1},{3,2},{4,7},{5,4},{6,5},{7,6},{8,11},{9,8},{10,9... | collective-permute-start | bytes 122888 | tf_op jit(solution)/shard_map/ppermute | solution.py:41
  108.6 0.4 collective-permute-start.12
  109.0 0.6 collective-permute-start.11
  109.6 0.7 collective-permute-done.13.refs_7_
  110.3 3.8 %collective-permute-done.12.refs_6_ = f32[80,128]{1,0:T(8,128)S(1)} collective-permute-done((f32[80,128]{1,0:T(8,128)S(1)}, f32[80,128]{1,0:T(8,128)S(1)}, u32[]{:S(2)}, u32[]{:S(2)}) %collective-permute-start.12) | collective-permute-done | bytes 40992 | tf_op jit(solution)/shard_map/ppermute | solution.py:41
  114.1 0.4 collective-permute-done.11.refs_5_
  114.6 1.0 last.1
  (12 shorter events, 0.1 us)
Async XLA Ops:
  0.6 1.5 %collective-permute-start = (f32[4,600]{1,0:T(4,128)}, f32[4,600]{1,0:T(4,128)S(1)}, u32[]{:S(2)}, u32[]{:S(2)}) collective-permute-start(f32[4,600]{1,0:T(4,128)} %bitcast.15), channel_id=1, source_target_pairs={{0,4},{4,0},{8,12},{12,8},{16,20},{20,16},{24,28},{28,24},{32,36},... | collective-permute-start | bytes 28808 | tf_op jit(solution)/shard_map/ppermute | solution.py:30
  0.7 2.1 %collective-permute-start.4 = (f32[4,1024]{1,0:T(4,128)}, f32[4,1024]{1,0:T(4,128)S(1)}, u32[]{:S(2)}, u32[]{:S(2)}) collective-permute-start(f32[4,1024]{1,0:T(4,128)} %refs_2_.4), channel_id=1, source_target_pairs={{0,4},{4,0},{8,12},{12,8},{16,20},{20,16},{24,28},{28,24},{32,36},... | collective-permute-start | bytes 49160 | tf_op jit(solution)/shard_map/ppermute | solution.py:30
  2.8 32.4 %slice-start = ((s8[9830400]{0:T(1024)(128)(4,1)}), s8[4194304]{0:T(1024)(128)(4,1)S(1)}, s32[]{:S(2)}) async-start(s8[9830400]{0:T(1024)(128)(4,1)} %bitcast.9), calls=%async_computation.4 | async-start | bytes 8388608
  2.8 8.9 %copy-start.1 = (f32[4,2,8,32]{3,2,1,0:T(8,128)S(1)}, f32[4,2,8,32]{3,2,1,0:T(8,128)}, u32[]{:S(2)}) copy-start(f32[4,2,8,32]{3,2,1,0:T(8,128)} %constant.17.clone.to_freq_ref.refs_2_) | copy-start | bytes 24580
  2.8 32.4 %slice-start.1 = ((s8[9830400]{0:T(1024)(128)(4,1)}), s8[4194304]{0:T(1024)(128)(4,1)S(1)}, s32[]{:S(2)}) async-start(s8[9830400]{0:T(1024)(128)(4,1)} %bitcast.9), calls=%async_computation.5 | async-start | bytes 8388608
  2.9 32.4 %slice-start.2 = ((s8[9830400]{0:T(1024)(128)(4,1)}), s8[1441792]{0:T(1024)(128)(4,1)S(1)}, s32[]{:S(2)}) async-start(s8[9830400]{0:T(1024)(128)(4,1)} %bitcast.9), calls=%async_computation.6 | async-start | bytes 2883584
  2.9 32.4 %copy-start.2 = (f32[4,1024]{1,0:T(4,128)S(1)}, f32[4,1024]{1,0:T(4,128)}, u32[]{:S(2)}) copy-start(f32[4,1024]{1,0:T(4,128)} %refs_2_.4) | copy-start | bytes 49156
  2.9 32.4 %collective-permute-start.5 = (bf16[2,4,600,1024]{3,2,1,0:T(8,128)(2,1)}, bf16[2,4,600,1024]{3,2,1,0:T(8,128)(2,1)S(1)}, u32[]{:S(2)}, u32[]{:S(2)}) collective-permute-start(bf16[2,4,600,1024]{3,2,1,0:T(8,128)(2,1)} %refs_0_.3), channel_id=1, source_target_pairs={{0,4},{4,0},{8,12},{12,8},{16,20},{20,16},{24,28},{28,24},{32,36},... | collective-permute-start | bytes 29491208 | tf_op jit(solution)/shard_map/ppermute | solution.py:30
  3.1 4.5 %collective-permute-start.3 = (f32[8,600]{1,0:T(8,128)S(1)}, f32[8,600]{1,0:T(8,128)S(1)}, u32[]{:S(2)}, u32[]{:S(2)}) collective-permute-start(f32[8,600]{1,0:T(8,128)S(1)} %pad_maximum_fusion.2.refs_0_.refs_5_), channel_id=1, source_target_pairs={{0,3},{1,0},{2,1},{3,2},{4,7},{5,4},{6,5},{7,6},{8,11},{9,8},{10,9... | collective-permute-start | bytes 57608 | tf_op jit(solution)/shard_map/ppermute | solution.py:41
  5.9 5.3 %collective-permute-start.2 = (f32[8,600]{1,0:T(8,128)S(1)}, f32[8,600]{1,0:T(8,128)S(1)}, u32[]{:S(2)}, u32[]{:S(2)}) collective-permute-start(f32[8,600]{1,0:T(8,128)S(1)} %pad_maximum_fusion.2.refs_0_.refs_5_), channel_id=1, source_target_pairs={{0,2},{1,3},{2,0},{3,1},{4,6},{5,7},{6,4},{7,5},{8,10},{9,11},{10,... | collective-permute-start | bytes 57608 | tf_op jit(solution)/shard_map/ppermute | solution.py:41
  6.7 5.0 %collective-permute-start.1 = (f32[8,600]{1,0:T(8,128)S(1)}, f32[8,600]{1,0:T(8,128)S(1)}, u32[]{:S(2)}, u32[]{:S(2)}) collective-permute-start(f32[8,600]{1,0:T(8,128)S(1)} %pad_maximum_fusion.2.refs_0_.refs_5_), channel_id=1, source_target_pairs={{0,1},{1,2},{2,3},{3,0},{4,5},{5,6},{6,7},{7,4},{8,9},{9,10},{10,1... | collective-permute-start | bytes 57608 | tf_op jit(solution)/shard_map/ppermute | solution.py:41
  35.3 30.7 %copy-start = (f32[4,2,32,64]{3,2,1,0:T(8,128)S(1)}, f32[4,2,32,64]{3,2,1,0:T(8,128)}, u32[]{:S(2)}) copy-start(f32[4,2,32,64]{3,2,1,0:T(8,128)} %constant.18.clone.refs_3_.to_time_ref) | copy-start | bytes 196612
  35.3 30.7 %copy-start.3 = (f32[600]{0:T(1024)S(1)}, f32[600]{0:T(1024)}, u32[]{:S(2)}) copy-start(f32[600]{0:T(1024)} %noise_ref.1) | copy-start | bytes 7204
  57.2 1.3 %collective-permute-start.6 = (f32[40,128]{1,0:T(8,128)S(1)}, f32[40,128]{1,0:T(8,128)S(1)}, u32[]{:S(2)}, u32[]{:S(2)}) collective-permute-start(f32[40,128]{1,0:T(8,128)S(1)} %convert_reduce_fusion.1), channel_id=1, source_target_pairs={{0,4},{4,0},{8,12},{12,8},{16,20},{20,16},{24,28},{28,24},{32,36},... | collective-permute-start | bytes 61448 | tf_op jit(solution)/shard_map/ppermute | solution.py:30
  58.5 4.2 %collective-permute-start.9 = (f32[80,128]{1,0:T(8,128)S(1)}, f32[80,128]{1,0:T(8,128)S(1)}, u32[]{:S(2)}, u32[]{:S(2)}) collective-permute-start(f32[80,128]{1,0:T(8,128)S(1)} %pad_maximum_fusion.refs_9_), channel_id=1, source_target_pairs={{0,3},{1,0},{2,1},{3,2},{4,7},{5,4},{6,5},{7,6},{8,11},{9,8},{10,9... | collective-permute-start | bytes 122888 | tf_op jit(solution)/shard_map/ppermute | solution.py:41
  59.7 5.8 %collective-permute-start.8 = (f32[80,128]{1,0:T(8,128)S(1)}, f32[80,128]{1,0:T(8,128)S(1)}, u32[]{:S(2)}, u32[]{:S(2)}) collective-permute-start(f32[80,128]{1,0:T(8,128)S(1)} %pad_maximum_fusion.refs_9_), channel_id=1, source_target_pairs={{0,2},{1,3},{2,0},{3,1},{4,6},{5,7},{6,4},{7,5},{8,10},{9,11},{10,... | collective-permute-start | bytes 122888 | tf_op jit(solution)/shard_map/ppermute | solution.py:41
  60.7 5.2 %collective-permute-start.7 = (f32[80,128]{1,0:T(8,128)S(1)}, f32[80,128]{1,0:T(8,128)S(1)}, u32[]{:S(2)}, u32[]{:S(2)}) collective-permute-start(f32[80,128]{1,0:T(8,128)S(1)} %pad_maximum_fusion.refs_9_), channel_id=1, source_target_pairs={{0,1},{1,2},{2,3},{3,0},{4,5},{5,6},{6,7},{7,4},{8,9},{9,10},{10,1... | collective-permute-start | bytes 122888 | tf_op jit(solution)/shard_map/ppermute | solution.py:41
  104.9 1.3 %collective-permute-start.10 = (f32[40,128]{1,0:T(8,128)S(1)}, f32[40,128]{1,0:T(8,128)S(1)}, u32[]{:S(2)}, u32[]{:S(2)}) collective-permute-start(f32[40,128]{1,0:T(8,128)S(1)} %convert_reduce_fusion), channel_id=1, source_target_pairs={{0,4},{4,0},{8,12},{12,8},{16,20},{20,16},{24,28},{28,24},{32,36},... | collective-permute-start | bytes 61448 | tf_op jit(solution)/shard_map/ppermute | solution.py:30
  106.2 4.1 %collective-permute-start.13 = (f32[80,128]{1,0:T(8,128)S(1)}, f32[80,128]{1,0:T(8,128)S(1)}, u32[]{:S(2)}, u32[]{:S(2)}) collective-permute-start(f32[80,128]{1,0:T(8,128)S(1)} %pad_maximum_fusion.1.refs_4_), channel_id=1, source_target_pairs={{0,3},{1,0},{2,1},{3,2},{4,7},{5,4},{6,5},{7,6},{8,11},{9,8},{10,9... | collective-permute-start | bytes 122888 | tf_op jit(solution)/shard_map/ppermute | solution.py:41
  108.6 5.5 %collective-permute-start.12 = (f32[80,128]{1,0:T(8,128)S(1)}, f32[80,128]{1,0:T(8,128)S(1)}, u32[]{:S(2)}, u32[]{:S(2)}) collective-permute-start(f32[80,128]{1,0:T(8,128)S(1)} %pad_maximum_fusion.1.refs_4_), channel_id=1, source_target_pairs={{0,2},{1,3},{2,0},{3,1},{4,6},{5,7},{6,4},{7,5},{8,10},{9,11},{10,... | collective-permute-start | bytes 122888 | tf_op jit(solution)/shard_map/ppermute | solution.py:41
  109.0 5.6 %collective-permute-start.11 = (f32[80,128]{1,0:T(8,128)S(1)}, f32[80,128]{1,0:T(8,128)S(1)}, u32[]{:S(2)}, u32[]{:S(2)}) collective-permute-start(f32[80,128]{1,0:T(8,128)S(1)} %pad_maximum_fusion.1.refs_4_), channel_id=1, source_target_pairs={{0,1},{1,2},{2,3},{3,0},{4,5},{5,6},{6,7},{7,4},{8,9},{9,10},{10,1... | collective-permute-start | bytes 122888 | tf_op jit(solution)/shard_map/ppermute | solution.py:41

commit v4 on v3

--- a/solution.py
+++ b/solution.py
@@ -16,13 +16,15 @@
 VMEM = pltpu.VMEM
 LANES = 128
 MIB = 1024 * 1024
+CHIP_ORDER = [
+    4, 22, 12, 28, 23, 17, 3, 25, 30, 9, 19, 26, 27, 21, 11, 7,
+    31, 10, 24, 16, 1, 5, 20, 8, 29, 14, 6, 0, 18, 15, 13, 2,
+]
 
 
 def one_core_groups(count):
-    size = count // 2
-    tall = 8
-    order = [(place % (size // tall)) * tall + place // (size // tall) for place in range(size)]
-    return [[2 * chip + core for chip in order] for core in range(2)]
+    assert sorted(CHIP_ORDER) == list(range(count // 2))
+    return [[2 * chip + core for chip in CHIP_ORDER] for core in range(2)]
 
 
 def from_other_core(value):

time: 117 us -> 113 us (0.966)
  blocking collectives: 73.1 us -> 70.1 us
    all_to_all x4, blocking collectives: 73.1 us -> 70.1 us  [exchange(): lax.all_to_all(blocks, 'param', 0, 0, axis_index_groups=groups, tiled=True)]
where the time goes in v4:
time: 113 us; the launch traced here: 112 us
  blocking collectives  70.1 us (62%)
  waiting for transfers between devices  16.4 us (15%)
  starting transfers between devices  12 us (11%)
  Pallas kernels  12 us (11%)
    all_to_all x4, blocking collectives, exchange(): lax.all_to_all(blocks, 'param', 0, 0, axis_index_groups=groups, tiled=True)  70.1 us
    ppermute x9, waiting for transfers between devices, freq_slots(): lax.ppermute(value, 'freq', [(i, (i + d) % length) for i in range(length)])  13.2 us
    pallas_call x6, Pallas kernels, vmem_call(): pl.pallas_call(body, out_shape=[jax.ShapeDtypeStruct(shape, dtype) for sh...  12 us
    ppermute x9, starting transfers between devices, freq_slots(): lax.ppermute(value, 'freq', [(i, (i + d) % length) for i in range(length)])  11 us
    ppermute x5, waiting for transfers between devices, from_other_core(): return lax.ppermute(value, 'param', [(i, i ^ 1) for i in range(count)])  3.23 us
  transfers between devices with their start and end apart: 14, of which 11 were waited for; matrix products, arithmetic and copies ran while one was open for 1% of the time, Pallas kernels for 0%

profile of v4, /device:TPU:32, one launch (start us, length us, event | category | flops | bytes accessed | tf_op | source)
XLA Modules:
  0.0 112.4 jit_solution(6818463908548994718)
XLA Ops:
  0.6 0.1 collective-permute-start
  0.7 0.5 collective-permute-start.4
  1.2 0.9 collective-permute-done
  2.1 0.7 pad_maximum_fusion.2.refs_0_.refs_5_
  2.8 0.0 collective-permute-done.4.refs_3_
  2.8 0.0 slice-start
  2.8 0.0 copy-start.1
  2.8 0.0 slice-start.1
  2.9 0.0 slice-start.2
  2.9 0.0 copy-start.2
  2.9 0.3 collective-permute-start.5
  3.1 2.8 %collective-permute-start.3 = (f32[8,600]{1,0:T(8,128)S(1)}, f32[8,600]{1,0:T(8,128)S(1)}, u32[]{:S(2)}, u32[]{:S(2)}) collective-permute-start(f32[8,600]{1,0:T(8,128)S(1)} %pad_maximum_fusion.2.refs_0_.refs_5_), channel_id=1, source_target_pairs={{0,3},{1,0},{2,1},{3,2},{4,7},{5,4},{6,5},{7,6},{8,11},{9,8},{10,9... | collective-permute-start | bytes 57608 | tf_op jit(solution)/shard_map/ppermute | solution.py:43
  5.9 0.8 collective-permute-start.2
  6.7 0.9 collective-permute-start.1
  7.6 0.0 collective-permute-done.3.refs_3_.refs_8_
  7.6 3.6 %collective-permute-done.2.refs_2_.refs_7_ = f32[8,600]{1,0:T(8,128)S(1)} collective-permute-done((f32[8,600]{1,0:T(8,128)S(1)}, f32[8,600]{1,0:T(8,128)S(1)}, u32[]{:S(2)}, u32[]{:S(2)}) %collective-permute-start.2) | collective-permute-done | bytes 19232 | tf_op jit(solution)/shard_map/ppermute | solution.py:43
  11.2 0.5 collective-permute-done.1.refs_1_.refs_6_
  11.7 0.0 copy-done.1
  11.7 0.2 first.1
  11.9 21.4 %all_to_all.20 = bf16[32,8,600]{2,1,0:T(8,128)(2,1)S(1)} all-to-all(bf16[32,8,600]{2,1,0:T(8,128)(2,1)S(1)} %first.1), channel_id=1, replica_groups={{32,176,96,224,184,136,24,200,240,72,152,208,216,168,88,56,248,80,192,1..., dimensions={0} | all-to-all | bytes 614400 | tf_op jit(solution)/shard_map/all_to_all | solution.py:37
  33.3 0.0 collective-permute-done.5.refs_1_
  33.3 0.0 copy-start
  33.4 0.0 copy-start.3
  33.4 5.1 %hessian.2 = f32[1280,128]{1,0:T(8,128)S(1)} custom-call(s32[1]{0:T(128)} %bitcast.1.refs_1_.core_ref, bf16[2,4,600,1024]{3,2,1,0:T(8,128)(2,1)S(1)} %bitcast.10, bf16[2,4,600,1024]{3,2,1,0:T(8,128)(2,1)S(1)} %collective-permute-done.5.refs_1_, f32[4,1024]{1,0:T(4,128)S(1)} %copy-done.2, f32[4,1024]{1,0:T(4,128)S(1)} %collective-permute-done.4.refs_3_, ...), custom_call_target="tpu_custom_call" | custom-call | tf_op jit(solution)/shard_map/hessian/pallas_call | solution.py:239
  38.5 16.1 %all_to_all.21 = bf16[32,40,128]{2,1,0:T(8,128)(2,1)S(1)} all-to-all(bf16[32,40,128]{2,1,0:T(8,128)(2,1)S(1)} %bitcast.13), channel_id=1, replica_groups={{32,176,96,224,184,136,24,200,240,72,152,208,216,168,88,56,248,80,192,1..., dimensions={0} | all-to-all | bytes 655360 | tf_op jit(solution)/shard_map/all_to_all | solution.py:37
  54.6 0.1 convert_reduce_fusion.1
  54.7 0.1 collective-permute-start.6
  54.8 1.2 %collective-permute-done.6 = f32[40,128]{1,0:T(8,128)S(1)} collective-permute-done((f32[40,128]{1,0:T(8,128)S(1)}, f32[40,128]{1,0:T(8,128)S(1)}, u32[]{:S(2)}, u32[]{:S(2)}) %collective-permute-start.6) | collective-permute-done | bytes 20512 | tf_op jit(solution)/shard_map/ppermute | solution.py:32
  55.9 1.2 %collective-permute-start.9 = (f32[80,128]{1,0:T(8,128)S(1)}, f32[80,128]{1,0:T(8,128)S(1)}, u32[]{:S(2)}, u32[]{:S(2)}) collective-permute-start(f32[80,128]{1,0:T(8,128)S(1)} %pad_maximum_fusion.refs_9_), channel_id=1, source_target_pairs={{0,3},{1,0},{2,1},{3,2},{4,7},{5,4},{6,5},{7,6},{8,11},{9,8},{10,9... | collective-permute-start | bytes 122888 | tf_op jit(solution)/shard_map/ppermute | solution.py:43
  57.1 0.9 collective-permute-start.8
  58.0 1.1 %collective-permute-start.7 = (f32[80,128]{1,0:T(8,128)S(1)}, f32[80,128]{1,0:T(8,128)S(1)}, u32[]{:S(2)}, u32[]{:S(2)}) collective-permute-start(f32[80,128]{1,0:T(8,128)S(1)} %pad_maximum_fusion.refs_9_), channel_id=1, source_target_pairs={{0,1},{1,2},{2,3},{3,0},{4,5},{5,6},{6,7},{7,4},{8,9},{9,10},{10,1... | collective-permute-start | bytes 122888 | tf_op jit(solution)/shard_map/ppermute | solution.py:43
  59.2 1.1 %collective-permute-done.9.refs_12_ = f32[80,128]{1,0:T(8,128)S(1)} collective-permute-done((f32[80,128]{1,0:T(8,128)S(1)}, f32[80,128]{1,0:T(8,128)S(1)}, u32[]{:S(2)}, u32[]{:S(2)}) %collective-permute-start.9) | collective-permute-done | bytes 40992 | tf_op jit(solution)/shard_map/ppermute | solution.py:43
  60.3 2.6 %collective-permute-done.8.refs_11_ = f32[80,128]{1,0:T(8,128)S(1)} collective-permute-done((f32[80,128]{1,0:T(8,128)S(1)}, f32[80,128]{1,0:T(8,128)S(1)}, u32[]{:S(2)}, u32[]{:S(2)}) %collective-permute-start.8) | collective-permute-done | bytes 40992 | tf_op jit(solution)/shard_map/ppermute | solution.py:43
  62.9 0.4 collective-permute-done.7.refs_10_
  63.3 0.6 middle.1
  64.0 16.7 %all_to_all.22 = bf16[32,8,600]{2,1,0:T(8,128)(2,1)S(1)} all-to-all(bf16[32,8,600]{2,1,0:T(8,128)(2,1)S(1)} %get-tuple-element.15), channel_id=1, replica_groups={{32,176,96,224,184,136,24,200,240,72,152,208,216,168,88,56,248,80,192,1..., dimensions={0} | all-to-all | bytes 614400 | tf_op jit(solution)/shard_map/all_to_all | solution.py:37
  80.7 5.1 %hessian.3 = f32[1280,128]{1,0:T(8,128)S(1)} custom-call(s32[1]{0:T(128)} %bitcast.1.refs_1_.core_ref, bf16[2,4,600,1024]{3,2,1,0:T(8,128)(2,1)S(1)} %bitcast.10, bf16[2,4,600,1024]{3,2,1,0:T(8,128)(2,1)S(1)} %collective-permute-done.5.refs_1_, f32[4,1024]{1,0:T(4,128)S(1)} %copy-done.2, f32[4,1024]{1,0:T(4,128)S(1)} %collective-permute-done.4.refs_3_, ...), custom_call_target="tpu_custom_call" | custom-call | tf_op jit(solution)/shard_map/hessian/pallas_call | solution.py:239
  85.8 16.0 %all_to_all.23 = bf16[32,40,128]{2,1,0:T(8,128)(2,1)S(1)} all-to-all(bf16[32,40,128]{2,1,0:T(8,128)(2,1)S(1)} %bitcast.14), channel_id=1, replica_groups={{32,176,96,224,184,136,24,200,240,72,152,208,216,168,88,56,248,80,192,1..., dimensions={0} | all-to-all | bytes 655360 | tf_op jit(solution)/shard_map/all_to_all | solution.py:37
  101.8 0.1 convert_reduce_fusion
  101.9 0.1 collective-permute-start.10
  102.0 1.2 %collective-permute-done.10 = f32[40,128]{1,0:T(8,128)S(1)} collective-permute-done((f32[40,128]{1,0:T(8,128)S(1)}, f32[40,128]{1,0:T(8,128)S(1)}, u32[]{:S(2)}, u32[]{:S(2)}) %collective-permute-start.10) | collective-permute-done | bytes 20512 | tf_op jit(solution)/shard_map/ppermute | solution.py:32
  103.1 2.4 %collective-permute-start.13 = (f32[80,128]{1,0:T(8,128)S(1)}, f32[80,128]{1,0:T(8,128)S(1)}, u32[]{:S(2)}, u32[]{:S(2)}) collective-permute-start(f32[80,128]{1,0:T(8,128)S(1)} %pad_maximum_fusion.1.refs_4_), channel_id=1, source_target_pairs={{0,3},{1,0},{2,1},{3,2},{4,7},{5,4},{6,5},{7,6},{8,11},{9,8},{10,9... | collective-permute-start | bytes 122888 | tf_op jit(solution)/shard_map/ppermute | solution.py:43
  105.5 0.2 collective-permute-start.12
  105.7 0.7 collective-permute-start.11
  106.5 0.7 collective-permute-done.13.refs_7_
  107.2 3.8 %collective-permute-done.12.refs_6_ = f32[80,128]{1,0:T(8,128)S(1)} collective-permute-done((f32[80,128]{1,0:T(8,128)S(1)}, f32[80,128]{1,0:T(8,128)S(1)}, u32[]{:S(2)}, u32[]{:S(2)}) %collective-permute-start.12) | collective-permute-done | bytes 40992 | tf_op jit(solution)/shard_map/ppermute | solution.py:43
  111.0 0.4 collective-permute-done.11.refs_5_
  111.4 1.0 last.1
  (12 shorter events, 0.1 us)
Async XLA Ops:
  0.6 1.5 %collective-permute-start = (f32[4,600]{1,0:T(4,128)}, f32[4,600]{1,0:T(4,128)S(1)}, u32[]{:S(2)}, u32[]{:S(2)}) collective-permute-start(f32[4,600]{1,0:T(4,128)} %bitcast.15), channel_id=1, source_target_pairs={{0,4},{4,0},{8,12},{12,8},{16,20},{20,16},{24,28},{28,24},{32,36},... | collective-permute-start | bytes 28808 | tf_op jit(solution)/shard_map/ppermute | solution.py:32
  0.7 2.1 %collective-permute-start.4 = (f32[4,1024]{1,0:T(4,128)}, f32[4,1024]{1,0:T(4,128)S(1)}, u32[]{:S(2)}, u32[]{:S(2)}) collective-permute-start(f32[4,1024]{1,0:T(4,128)} %refs_2_.4), channel_id=1, source_target_pairs={{0,4},{4,0},{8,12},{12,8},{16,20},{20,16},{24,28},{28,24},{32,36},... | collective-permute-start | bytes 49160 | tf_op jit(solution)/shard_map/ppermute | solution.py:32
  2.8 30.5 %slice-start = ((s8[9830400]{0:T(1024)(128)(4,1)}), s8[4194304]{0:T(1024)(128)(4,1)S(1)}, s32[]{:S(2)}) async-start(s8[9830400]{0:T(1024)(128)(4,1)} %bitcast.9), calls=%async_computation.4 | async-start | bytes 8388608
  2.8 8.9 %copy-start.1 = (f32[4,2,8,32]{3,2,1,0:T(8,128)S(1)}, f32[4,2,8,32]{3,2,1,0:T(8,128)}, u32[]{:S(2)}) copy-start(f32[4,2,8,32]{3,2,1,0:T(8,128)} %constant.17.clone.to_freq_ref.refs_2_) | copy-start | bytes 24580
  2.8 30.5 %slice-start.1 = ((s8[9830400]{0:T(1024)(128)(4,1)}), s8[4194304]{0:T(1024)(128)(4,1)S(1)}, s32[]{:S(2)}) async-start(s8[9830400]{0:T(1024)(128)(4,1)} %bitcast.9), calls=%async_computation.5 | async-start | bytes 8388608
  2.9 30.5 %slice-start.2 = ((s8[9830400]{0:T(1024)(128)(4,1)}), s8[1441792]{0:T(1024)(128)(4,1)S(1)}, s32[]{:S(2)}) async-start(s8[9830400]{0:T(1024)(128)(4,1)} %bitcast.9), calls=%async_computation.6 | async-start | bytes 2883584
  2.9 30.5 %copy-start.2 = (f32[4,1024]{1,0:T(4,128)S(1)}, f32[4,1024]{1,0:T(4,128)}, u32[]{:S(2)}) copy-start(f32[4,1024]{1,0:T(4,128)} %refs_2_.4) | copy-start | bytes 49156
  2.9 30.4 %collective-permute-start.5 = (bf16[2,4,600,1024]{3,2,1,0:T(8,128)(2,1)}, bf16[2,4,600,1024]{3,2,1,0:T(8,128)(2,1)S(1)}, u32[]{:S(2)}, u32[]{:S(2)}) collective-permute-start(bf16[2,4,600,1024]{3,2,1,0:T(8,128)(2,1)} %refs_0_.3), channel_id=1, source_target_pairs={{0,4},{4,0},{8,12},{12,8},{16,20},{20,16},{24,28},{28,24},{32,36},... | collective-permute-start | bytes 29491208 | tf_op jit(solution)/shard_map/ppermute | solution.py:32
  3.1 4.5 %collective-permute-start.3 = (f32[8,600]{1,0:T(8,128)S(1)}, f32[8,600]{1,0:T(8,128)S(1)}, u32[]{:S(2)}, u32[]{:S(2)}) collective-permute-start(f32[8,600]{1,0:T(8,128)S(1)} %pad_maximum_fusion.2.refs_0_.refs_5_), channel_id=1, source_target_pairs={{0,3},{1,0},{2,1},{3,2},{4,7},{5,4},{6,5},{7,6},{8,11},{9,8},{10,9... | collective-permute-start | bytes 57608 | tf_op jit(solution)/shard_map/ppermute | solution.py:43
  5.9 5.3 %collective-permute-start.2 = (f32[8,600]{1,0:T(8,128)S(1)}, f32[8,600]{1,0:T(8,128)S(1)}, u32[]{:S(2)}, u32[]{:S(2)}) collective-permute-start(f32[8,600]{1,0:T(8,128)S(1)} %pad_maximum_fusion.2.refs_0_.refs_5_), channel_id=1, source_target_pairs={{0,2},{1,3},{2,0},{3,1},{4,6},{5,7},{6,4},{7,5},{8,10},{9,11},{10,... | collective-permute-start | bytes 57608 | tf_op jit(solution)/shard_map/ppermute | solution.py:43
  6.7 5.0 %collective-permute-start.1 = (f32[8,600]{1,0:T(8,128)S(1)}, f32[8,600]{1,0:T(8,128)S(1)}, u32[]{:S(2)}, u32[]{:S(2)}) collective-permute-start(f32[8,600]{1,0:T(8,128)S(1)} %pad_maximum_fusion.2.refs_0_.refs_5_), channel_id=1, source_target_pairs={{0,1},{1,2},{2,3},{3,0},{4,5},{5,6},{6,7},{7,4},{8,9},{9,10},{10,1... | collective-permute-start | bytes 57608 | tf_op jit(solution)/shard_map/ppermute | solution.py:43
  33.3 30.0 %copy-start = (f32[4,2,32,64]{3,2,1,0:T(8,128)S(1)}, f32[4,2,32,64]{3,2,1,0:T(8,128)}, u32[]{:S(2)}) copy-start(f32[4,2,32,64]{3,2,1,0:T(8,128)} %constant.18.clone.refs_3_.to_time_ref) | copy-start | bytes 196612
  33.4 30.0 %copy-start.3 = (f32[600]{0:T(1024)S(1)}, f32[600]{0:T(1024)}, u32[]{:S(2)}) copy-start(f32[600]{0:T(1024)} %noise_ref.1) | copy-start | bytes 7204
  54.7 1.3 %collective-permute-start.6 = (f32[40,128]{1,0:T(8,128)S(1)}, f32[40,128]{1,0:T(8,128)S(1)}, u32[]{:S(2)}, u32[]{:S(2)}) collective-permute-start(f32[40,128]{1,0:T(8,128)S(1)} %convert_reduce_fusion.1), channel_id=1, source_target_pairs={{0,4},{4,0},{8,12},{12,8},{16,20},{20,16},{24,28},{28,24},{32,36},... | collective-permute-start | bytes 61448 | tf_op jit(solution)/shard_map/ppermute | solution.py:32
  55.9 4.3 %collective-permute-start.9 = (f32[80,128]{1,0:T(8,128)S(1)}, f32[80,128]{1,0:T(8,128)S(1)}, u32[]{:S(2)}, u32[]{:S(2)}) collective-permute-start(f32[80,128]{1,0:T(8,128)S(1)} %pad_maximum_fusion.refs_9_), channel_id=1, source_target_pairs={{0,3},{1,0},{2,1},{3,2},{4,7},{5,4},{6,5},{7,6},{8,11},{9,8},{10,9... | collective-permute-start | bytes 122888 | tf_op jit(solution)/shard_map/ppermute | solution.py:43
  57.1 5.8 %collective-permute-start.8 = (f32[80,128]{1,0:T(8,128)S(1)}, f32[80,128]{1,0:T(8,128)S(1)}, u32[]{:S(2)}, u32[]{:S(2)}) collective-permute-start(f32[80,128]{1,0:T(8,128)S(1)} %pad_maximum_fusion.refs_9_), channel_id=1, source_target_pairs={{0,2},{1,3},{2,0},{3,1},{4,6},{5,7},{6,4},{7,5},{8,10},{9,11},{10,... | collective-permute-start | bytes 122888 | tf_op jit(solution)/shard_map/ppermute | solution.py:43
  58.0 5.3 %collective-permute-start.7 = (f32[80,128]{1,0:T(8,128)S(1)}, f32[80,128]{1,0:T(8,128)S(1)}, u32[]{:S(2)}, u32[]{:S(2)}) collective-permute-start(f32[80,128]{1,0:T(8,128)S(1)} %pad_maximum_fusion.refs_9_), channel_id=1, source_target_pairs={{0,1},{1,2},{2,3},{3,0},{4,5},{5,6},{6,7},{7,4},{8,9},{9,10},{10,1... | collective-permute-start | bytes 122888 | tf_op jit(solution)/shard_map/ppermute | solution.py:43
  101.9 1.3 %collective-permute-start.10 = (f32[40,128]{1,0:T(8,128)S(1)}, f32[40,128]{1,0:T(8,128)S(1)}, u32[]{:S(2)}, u32[]{:S(2)}) collective-permute-start(f32[40,128]{1,0:T(8,128)S(1)} %convert_reduce_fusion), channel_id=1, source_target_pairs={{0,4},{4,0},{8,12},{12,8},{16,20},{20,16},{24,28},{28,24},{32,36},... | collective-permute-start | bytes 61448 | tf_op jit(solution)/shard_map/ppermute | solution.py:32
  103.1 4.0 %collective-permute-start.13 = (f32[80,128]{1,0:T(8,128)S(1)}, f32[80,128]{1,0:T(8,128)S(1)}, u32[]{:S(2)}, u32[]{:S(2)}) collective-permute-start(f32[80,128]{1,0:T(8,128)S(1)} %pad_maximum_fusion.1.refs_4_), channel_id=1, source_target_pairs={{0,3},{1,0},{2,1},{3,2},{4,7},{5,4},{6,5},{7,6},{8,11},{9,8},{10,9... | collective-permute-start | bytes 122888 | tf_op jit(solution)/shard_map/ppermute | solution.py:43
  105.5 5.5 %collective-permute-start.12 = (f32[80,128]{1,0:T(8,128)S(1)}, f32[80,128]{1,0:T(8,128)S(1)}, u32[]{:S(2)}, u32[]{:S(2)}) collective-permute-start(f32[80,128]{1,0:T(8,128)S(1)} %pad_maximum_fusion.1.refs_4_), channel_id=1, source_target_pairs={{0,2},{1,3},{2,0},{3,1},{4,6},{5,7},{6,4},{7,5},{8,10},{9,11},{10,... | collective-permute-start | bytes 122888 | tf_op jit(solution)/shard_map/ppermute | solution.py:43
  105.7 5.7 %collective-permute-start.11 = (f32[80,128]{1,0:T(8,128)S(1)}, f32[80,128]{1,0:T(8,128)S(1)}, u32[]{:S(2)}, u32[]{:S(2)}) collective-permute-start(f32[80,128]{1,0:T(8,128)S(1)} %pad_maximum_fusion.1.refs_4_), channel_id=1, source_target_pairs={{0,1},{1,2},{2,3},{3,0},{4,5},{5,6},{6,7},{7,4},{8,9},{9,10},{10,1... | collective-permute-start | bytes 122888 | tf_op jit(solution)/shard_map/ppermute | solution.py:43
